TPU v7x, 512 devices: a whole 4x8x8 slice. The times are simulated.
512 devices in a mesh: seq: 32 (over x_hi, y, core), doc: 16 (over x_lo, z).
Axes of the slice: x: 4 (x_hi: 2, x_lo: 2; x = x_hi * 2 + x_lo), y: 8, z: 8, core: 2. Of those that a mesh axis runs over, the one named last changes fastest.
Arguments:
- hidden: bfloat16 [16, 4096, 768], P('doc', 'seq'), may hold values from -3 to 3
- queries: bfloat16 [16, 4096, 768], P('doc', 'seq'), may hold values from -8 to 8
- key_states: bfloat16 [16, 4096, 768], P('doc', 'seq'), may hold values from -8 to 8
- values: bfloat16 [16, 4096, 768], P('doc', 'seq'), may hold values from -8 to 8
- targets: int32 [16, 4096], P('doc', 'seq'), may hold values from 0 to 26623
- lengths: int32 [16], replicated, may hold values from 2048 to 4096
- keep_rank: int32 [1], replicated, may hold values from 0 to 99
- out_weight: bfloat16 [768, 768], replicated, may hold values from -0.21875 to 0.21875
- final_gain: float32 [768], replicated, may hold values from 0.5 to 1.5
- unembed: bfloat16 [768, 26624], P(None, 'doc'), may hold values from -0.390625 to 0.390625
Outputs:
- token_nll: float32 [16, 4096], P('doc', 'seq')
- log_perplexity: float32 [16], replicated
- acceptance: float32 [16], replicated
All inputs are finite; a program needn't handle non-finite values.
Results may differ from a plain program's by a relative error of at most 0.007.
Values may be sent and summed in bfloat16 or wider, within the bound.
A program may use at most 64 MiB of HBM per device.

v0:
```python
import math

import jax
import jax.numpy as jnp
from jax import lax
from jax.sharding import Mesh
from jax.sharding import PartitionSpec as P

HEADS = 12
HEAD_DIM = 64
ROT = 16
DOC = ("doc_0", "doc_1")


NEGATIVE = -1e30
ROTARY_BASE = 10000.0
NORM_EPSILON = 1e-05
SPREAD_EPSILON = 0.0001


def in_order(blocks, dim):
    blocks = jnp.moveaxis(blocks, 0, dim)
    shape = blocks.shape
    return blocks.reshape(*shape[:dim], shape[dim] * shape[dim + 1], *shape[dim + 2 :])


def all_blocks(array, axes, turns):
    blocks = array[None]
    for k in turns:
        blocks = lax.all_gather(blocks, axes[k], axis=0, tiled=True)
    held = [lax.axis_size(axes[k]) for k in reversed(turns)]
    blocks = blocks.reshape(*held, *array.shape)
    turned = sorted(range(len(turns)), key=lambda place: turns[len(turns) - 1 - place])
    return blocks.transpose(*turned, *range(len(turns), blocks.ndim)).reshape(-1, *array.shape)


def gathered_by_axis(array, axes, turns, dim):
    return in_order(all_blocks(array, axes, turns), dim)


def from_everyone(array, axis):
    copies = jnp.broadcast_to(array, (lax.axis_size(axis), *array.shape))
    return lax.all_to_all(copies, axis, split_axis=0, concat_axis=0, tiled=True)


def collected_together(array, axis):
    leaves = jax.tree.leaves(array)
    turns = sorted(range(len(leaves)), key=lambda k: -leaves[k].size)
    width = (1, *leaves[turns[0]].shape)[-1]
    lines = [
        jnp.pad(leaves[k].reshape(-1), (0, -leaves[k].size % width)).reshape(-1, width)
        for k in turns
    ]
    both, at, found = (from_everyone(jnp.concatenate(lines), axis), 0, {})
    for k, line in zip(turns, lines):
        piece = both[:, at : at + len(line)].reshape(len(both), -1)
        found[k] = piece[:, : leaves[k].size].reshape(-1, *leaves[k].shape)
        at += len(line)
    numbers = iter(range(len(leaves)))
    return jax.tree.map(lambda _: found[next(numbers)], array)


def folded_in_pairs(pieces, combine):
    while len(jax.tree.leaves(pieces)[0]) > 1:
        pieces = jax.vmap(combine)(
            *(jax.tree.map(lambda part: part[side::2], pieces) for side in (0, 1))
        )
    return jax.tree.map(lambda part: part[0], pieces)


def joined_all(array, axis, combine):
    pieces = collected_together(array, axis)
    return folded_in_pairs(pieces, combine)


def over_copies(array, axis):
    everything = from_everyone(array, axis)
    return jnp.sum(everything, axis=0)


def rotate(block, first_row):
    row_count = block.shape[0]
    half_rot = ROT // 2
    where_at = (first_row + jnp.arange(row_count, dtype=jnp.int32)).astype(jnp.float32)
    inv_freq = ROTARY_BASE ** (
        -2.0 * jnp.arange(half_rot, dtype=jnp.int32).astype(jnp.float32) / ROT
    )
    angles = where_at[:, None] * inv_freq[None, :]
    cosine = jnp.cos(angles)[:, None, :]
    sine_part = jnp.sin(angles)[:, None, :]
    per_head = block.reshape(row_count, HEADS, HEAD_DIM)
    low_half = per_head[:, :, :half_rot]
    high_half = per_head[:, :, half_rot:ROT]
    turned = jnp.concatenate(
        [
            low_half * cosine - high_half * sine_part,
            high_half * cosine + low_half * sine_part,
            per_head[:, :, ROT:],
        ],
        axis=2,
    )
    return turned.reshape(row_count, HEADS * HEAD_DIM)


def combine(first_part, second_part):
    top_first, total_first, pick_first = first_part
    top_second, total_second, pick_second = second_part
    top_score = jnp.maximum(top_first, top_second)
    merged = total_first * jnp.exp(top_first - top_score) + total_second * jnp.exp(
        top_second - top_score
    )
    return (top_score, merged, pick_first + pick_second)


def accept(log_perplexity, keep_rank):
    doc_count = log_perplexity.shape[0]
    center = log_perplexity - jnp.mean(log_perplexity)
    spread = jnp.sqrt(jnp.mean(center * center) + SPREAD_EPSILON)
    ordered = jnp.sort(log_perplexity)
    scaled_rank = keep_rank[0] * (doc_count - 1)
    low_index = scaled_rank // 99
    high_index = jnp.minimum(low_index + 1, doc_count - 1)
    fraction = (scaled_rank - 99 * low_index).astype(jnp.float32) / 99.0
    places = jnp.arange(doc_count, dtype=jnp.int32)
    low_value = jnp.sum(jnp.where(places == low_index, ordered, 0.0))
    high_value = jnp.sum(jnp.where(places == high_index, ordered, 0.0))
    rank_level = (1.0 - fraction) * low_value + fraction * high_value
    return jax.nn.sigmoid((rank_level - log_perplexity) / spread)


def shards(
    hidden,
    queries,
    key_states,
    values,
    targets,
    lengths,
    keep_rank,
    out_weight,
    final_gain,
    unembed,
):
    tok_rows = queries.shape[1]
    seq_index = lax.axis_index("seq")
    first_row = seq_index * tok_rows
    turned_q = rotate(queries[0].astype(jnp.float32), first_row).astype(jnp.bfloat16)
    turned_k = rotate(key_states[0].astype(jnp.float32), first_row).astype(jnp.bfloat16)
    query_heads = turned_q.reshape(tok_rows, HEADS, HEAD_DIM)
    query_place = first_row + jnp.arange(tok_rows, dtype=jnp.int32)
    last_row = first_row + tok_rows - 1
    score_scale = 1.0 / math.sqrt(HEAD_DIM)
    key_value = jnp.stack([turned_k, values[0]])
    start_state = (
        jnp.full((HEADS, tok_rows), NEGATIVE, jnp.float32),
        jnp.zeros((HEADS, tok_rows), jnp.float32),
        jnp.zeros((HEADS, tok_rows, HEAD_DIM), jnp.float32),
    )

    def absorb(running, pair_block, begin_at):
        row_count = pair_block.shape[1]
        key_heads = pair_block[0].reshape(row_count, HEADS, HEAD_DIM)
        value_heads = pair_block[1].reshape(row_count, HEADS, HEAD_DIM)
        scores = (
            jnp.einsum("qhd,khd->hqk", query_heads, key_heads, preferred_element_type=jnp.float32)
            * score_scale
        )
        key_place = begin_at + jnp.arange(row_count, dtype=jnp.int32)
        allowed = key_place[None, None, :] <= query_place[None, :, None]
        scores = jnp.where(allowed, scores, NEGATIVE)
        old_top, totals, summed = running
        top_score = jnp.maximum(old_top, jnp.max(scores, axis=2))
        weights = jnp.where(allowed, jnp.exp(scores - top_score[:, :, None]), 0.0)
        factor = jnp.exp(old_top - top_score)
        totals = totals * factor + jnp.sum(weights, axis=2)
        summed = summed * factor[:, :, None] + jnp.einsum(
            "hqk,khd->hqd",
            weights.astype(jnp.bfloat16),
            value_heads,
            preferred_element_type=jnp.float32,
        )
        return (top_score, totals, summed)

    shard_piece = lax.all_gather(key_value, "seq", axis=1, tiled=True)
    row_count = shard_piece.shape[1]
    fold_block_rows = math.gcd(row_count, 512)

    def inner_step(block_index, inner_state):
        part_block = lax.dynamic_slice_in_dim(
            shard_piece, block_index * fold_block_rows, fold_block_rows, 1
        )
        block_begin = block_index * fold_block_rows
        return lax.cond(
            block_begin <= last_row,
            lambda state_now: absorb(state_now, part_block, block_begin),
            lambda state_now: state_now,
            inner_state,
        )

    running = lax.fori_loop(0, row_count // fold_block_rows, inner_step, start_state)
    top_final, total_final, summed_final = running
    attended = (
        jnp.transpose(summed_final / total_final[:, :, None], (1, 0, 2))
        .reshape(tok_rows, HEADS * HEAD_DIM)
        .astype(jnp.bfloat16)
    )
    residual = hidden[0].astype(jnp.float32) + jnp.dot(
        attended, out_weight, preferred_element_type=jnp.float32
    )
    center = residual - jnp.mean(residual, axis=1, keepdims=True)
    spread = jnp.mean(center * center, axis=1, keepdims=True)
    normed = (center * lax.rsqrt(spread + NORM_EPSILON) * final_gain).astype(jnp.bfloat16)
    gathered_rows, gathered_targets = (
        gathered_by_axis(normed[None], DOC, (0, 1), 0),
        gathered_by_axis(targets, DOC, (0, 1), 0),
    )
    doc_count = gathered_rows.shape[0]
    row_total = doc_count * tok_rows
    flat_rows = gathered_rows.reshape(row_total, HEADS * HEAD_DIM)
    flat_targets = gathered_targets.reshape(row_total)
    vocab_share = unembed.shape[1]
    doc_index = lax.axis_index(DOC)
    offset = doc_index * vocab_share
    block_rows = math.gcd(row_total, 512)

    def shard_stats(block_index):
        begin_at = block_index * block_rows
        block = lax.dynamic_slice_in_dim(flat_rows, begin_at, block_rows, 0)
        logits = jnp.dot(block, unembed, preferred_element_type=jnp.float32)
        top_score = jnp.max(logits, axis=1)
        totals = jnp.sum(jnp.exp(logits - top_score[:, None]), axis=1)
        wanted = lax.dynamic_slice_in_dim(flat_targets, begin_at, block_rows, 0) - offset
        matches = jnp.arange(vocab_share, dtype=jnp.int32)[None, :] == wanted[:, None]
        picked = jnp.sum(jnp.where(matches, logits, 0.0), axis=1)
        return (top_score, totals, picked)

    tops, totals, picks = lax.map(shard_stats, jnp.arange(row_total // block_rows, dtype=jnp.int32))
    tops = tops.reshape(doc_count, tok_rows)
    totals = totals.reshape(doc_count, tok_rows)
    picks = picks.reshape(doc_count, tok_rows)
    top_all, total_all, pick_all = joined_all((tops, totals, picks), DOC, combine)
    is_valid = query_place[None, :] < lengths[:, None]
    token_all = jnp.where(is_valid, top_all + jnp.log(total_all) - pick_all, 0.0)
    doc_sums = over_copies(jnp.sum(token_all, axis=1), "seq")
    log_perplexity = doc_sums / lengths.astype(jnp.float32)
    token_own = lax.dynamic_slice_in_dim(token_all, doc_index, 1, 0)
    acceptance = accept(log_perplexity, keep_rank)
    return (token_own, log_perplexity, acceptance)


def solution(mesh):
    split = Mesh(mesh.devices.reshape(mesh.shape["seq"], 2, 8), ("seq", "doc_0", "doc_1"))
    placed = (
        P(DOC, "seq", None),
        P(DOC, "seq", None),
        P(DOC, "seq", None),
        P(DOC, "seq", None),
        P(DOC, "seq"),
        P(),
        P(),
        P(),
        P(),
        P(None, DOC),
    )
    return jax.shard_map(
        shards, mesh=split, in_specs=placed, out_specs=(P(DOC, "seq"), P(), P()), check_vma=False
    )
```

profile of v0, /device:TPU:1, one launch (start us, length us, event | category | flops | bytes accessed | tf_op | source)
XLA Modules:
  0.0 322.7 jit_solution(12917053944295169730)
XLA Ops:
  7.2 1.2 copy.39
  8.5 1.1 copy.41
  9.6 1.1 copy.40
  10.9 0.8 pad_maximum_fusion
  11.8 140.8 %all-gather.8.cloned.1.call-done = bf16[2,4096,768]{1,2,0:T(8,128)(2,1)} async-done(((bf16[2,128,768]{1,2,0:T(8,128)(2,1)}), bf16[2,4096,768]{1,2,0:T(8,128)(2,1)}) %all-gather.8.cloned.1.call-update) | async-done | bytes 12582928 | tf_op jit(solution)/shard_map/all_gather | solution.py:183
  152.7 4.8 %while.33 = (s32[]{:T(128)}, f32[12,128]{1,0:T(8,128)S(1)}, f32[12,128]{1,0:T(8,128)S(1)}, f32[12,128,64]{1,2,0:T(8,128)S(1)}, s32[]{:T(128)}, /*index=5*/bf16[2...) while((s32[]{:T(128)}, f32[12,128]{1,0:T(8,128)S(1)}, ...), condition=%wide.region_5.6_spmd.clone, body=%wide.region_0.5_spmd.clone.sunk | while | flops 211816064 | bytes 15505717 | solution.py:199
  152.8 4.4 %conditional.3 = ((f32[12,128]{1,0:T(8,128)S(1)}, f32[12,128]{1,0:T(8,128)S(1)}, f32[12,128,64]{1,2,0:T(8,128)S(1)})) conditional(s32[]{:T(128)} %convert_element_type.107, (f32[12,128]{1,0:T(8,128)S(1)}, f32[12,128]{1,0:T(8,128)S(1)}, f32[12,128,64]{1,2,0:T(8,128)S(1)}) %tuple.89, (s32[]{:T(128)}, s32[]{:T(128)}, bf16[2,4096,768]{1,2,0:T(8,128)(2,1)}, ...), branch_computations={%region_1.0_spmd, %region_2.4_spmd} | conditional | flops 211816064 | bytes 15504990 | solution.py:192
  152.8 1.5 constant_dynamic-slice_fusion.1
  154.5 0.8 fusion.2
  155.3 0.7 fusion.4
  156.0 1.1 fusion.8
  158.5 7.0 %all-gather = bf16[256,768]{1,0:T(8,128)(2,1)} all-gather(bf16[128,768]{1,0:T(8,128)(2,1)S(1)} %multiply_convert_fusion), channel_id=2, replica_groups=mesh['seq'=32,'doc_0'=2,'doc_1'=8] {'doc_0'}, dimensions={0}, use_global_device_ids=true | all-gather | bytes 589824 | tf_op jit(solution)/shard_map/all_gather | solution.py:30
  165.5 3.1 all-gather.3
  168.6 13.5 %all-gather.4 = s32[8,2,128]{2,1,0:T(2,128)S(1)} all-gather(s32[1,2,128]{2,1,0:T(2,128)S(1)} %bitcast.81), channel_id=4, replica_groups=mesh['seq'=32,'doc_0'=2,'doc_1'=8] {'doc_1'}, dimensions={0}, use_global_device_ids=true | all-gather | bytes 9216 | tf_op jit(solution)/shard_map/all_gather | solution.py:30
  182.1 59.3 %all-gather.10.cloned.1.call-done = bf16[16,1,128,768]{3,2,1,0:T(8,128)(2,1)} async-done(((bf16[2,1,128,768]{3,2,1,0:T(8,128)(2,1)}), bf16[16,1,128,768]{3,2,1,0:T(8,128)(2,1)}) %all-gather.10.cloned.1.call-update) | async-done | bytes 3145744 | tf_op jit(solution)/shard_map/all_gather | solution.py:30
  241.4 3.9 %copy.43 = bf16[2,8,1,128,768]{4,3,1,0,2:T(8,128)(2,1)} copy(bf16[2,8,1,128,768]{4,3,0,1,2:T(8,128)(2,1)} %bitcast.69) | data formatting | bytes 6291456 | tf_op jit(solution)/shard_map/transpose | solution.py:34
  245.3 25.4 %while.32 = (s32[]{:T(128)}, f32[4,512]{1,0:T(4,128)S(1)}, f32[4,512]{1,0:T(4,128)S(1)}, f32[4,512]{1,0:T(4,128)S(1)}, s32[4]{0:T(128)S(1)}, /*index=5*/bf16[204...) while((s32[]{:T(128)}, f32[4,512]{1,0:T(4,128)S(1)}, ...), condition=%wide.region_12.13_spmd, body=%wide.region_8.12_spmd.sunk | while | flops 1313733632 | bytes 10184911 | solution.py:236
  246.5 3.7 %fusion.42 = (f32[512]{0:T(512)S(1)}, f32[512,1664]{1,0:T(8,128)S(1)}) fusion(bf16[768,1664]{1,0:T(8,128)(2,1)} %get-tuple-element.568, bf16[2048,768]{1,0:T(8,128)(2,1)} %get-tuple-element.567, s32[]{:T(128)S(6)} %select_n.101), kind=kOutput, calls=%fused_computation.76.clone.1 | convolution fusion | flops 1309474304 | bytes 6752260 | tf_op jit(solution)/shard_map/while/body/eval_jaxpr/dot_general | solution.py:228
  250.3 1.2 select_reduce_fusion.2
  252.9 3.7 %fusion.42 = (f32[512]{0:T(512)S(1)}, f32[512,1664]{1,0:T(8,128)S(1)}) fusion(bf16[768,1664]{1,0:T(8,128)(2,1)} %get-tuple-element.568, bf16[2048,768]{1,0:T(8,128)(2,1)} %get-tuple-element.567, s32[]{:T(128)S(6)} %select_n.101), kind=kOutput, calls=%fused_computation.76.clone.1 | convolution fusion | flops 1309474304 | bytes 6752260 | tf_op jit(solution)/shard_map/while/body/eval_jaxpr/dot_general | solution.py:228
  256.6 1.2 select_reduce_fusion.2
  259.2 3.7 %fusion.42 = (f32[512]{0:T(512)S(1)}, f32[512,1664]{1,0:T(8,128)S(1)}) fusion(bf16[768,1664]{1,0:T(8,128)(2,1)} %get-tuple-element.568, bf16[2048,768]{1,0:T(8,128)(2,1)} %get-tuple-element.567, s32[]{:T(128)S(6)} %select_n.101), kind=kOutput, calls=%fused_computation.76.clone.1 | convolution fusion | flops 1309474304 | bytes 6752260 | tf_op jit(solution)/shard_map/while/body/eval_jaxpr/dot_general | solution.py:228
  263.0 1.2 select_reduce_fusion.2
  265.6 3.7 %fusion.42 = (f32[512]{0:T(512)S(1)}, f32[512,1664]{1,0:T(8,128)S(1)}) fusion(bf16[768,1664]{1,0:T(8,128)(2,1)} %get-tuple-element.568, bf16[2048,768]{1,0:T(8,128)(2,1)} %get-tuple-element.567, s32[]{:T(128)S(6)} %select_n.101), kind=kOutput, calls=%fused_computation.76.clone.1 | convolution fusion | flops 1309474304 | bytes 6752260 | tf_op jit(solution)/shard_map/while/body/eval_jaxpr/dot_general | solution.py:228
  269.3 1.2 select_reduce_fusion.2
  270.8 0.8 broadcast_in_dim.91
  271.5 4.9 %all-to-all-start = ((f32[16,48,128]{2,1,0:T(8,128)}), f32[16,48,128]{2,1,0:T(8,128)S(1)}, u32[]{:S(2)}, u32[]{:S(2)}) async-start(f32[16,48,128]{2,1,0:T(8,128)} %broadcast_in_dim.91), calls=%async_computation | async-start | bytes 786432 | tf_op jit(solution)/shard_map/all_to_all | solution.py:43
  277.1 10.4 %all-to-all-done = f32[16,48,128]{2,1,0:T(8,128)S(1)} async-done(((f32[16,48,128]{2,1,0:T(8,128)}), f32[16,48,128]{2,1,0:T(8,128)S(1)}, u32[]{:S(2)}, u32[]{:S(2)}) %all-to-all-start) | async-done | bytes 393248 | tf_op jit(solution)/shard_map/all_to_all | solution.py:43
  288.4 11.5 %all-to-all-start.1 = ((f32[32,1,16]{2,1,0:T(1,128)}), f32[32,1,16]{2,1,0:T(1,128)S(1)}, u32[]{:S(2)}, u32[]{:S(2)}) async-start(f32[32,1,16]{2,1,0:T(1,128)} %broadcast_in_dim.93), calls=%async_computation.1 | async-start | bytes 32768 | tf_op jit(solution)/shard_map/all_to_all | solution.py:43
  300.5 8.9 %all-to-all-done.1 = f32[32,1,16]{2,1,0:T(1,128)S(1)} async-done(((f32[32,1,16]{2,1,0:T(1,128)}), f32[32,1,16]{2,1,0:T(1,128)S(1)}, u32[]{:S(2)}, u32[]{:S(2)}) %all-to-all-start.1) | async-done | bytes 2080 | tf_op jit(solution)/shard_map/all_to_all | solution.py:43
  310.0 1.4 sort.15
  311.4 0.7 fusion.25
  (100 shorter events, 8.1 us)
Async XLA Ops:
  7.2 150.5 %copy-start = (bf16[768,768]{1,0:T(8,128)(2,1)S(1)}, bf16[768,768]{1,0:T(8,128)(2,1)}, u32[]{:S(2)}) copy-start(bf16[768,768]{1,0:T(8,128)(2,1)} %param.23) | copy-start | bytes 3538948
  7.2 145.5 %all-gather.8.cloned.1.call-start = ((), (), s32[]{:S(2)}) async-start(), calls=%async_computation.2 | async-start | bytes 12976128 | tf_op jit(solution)/shard_map/all_gather | solution.py:183
  11.7 229.7 %all-gather.10.cloned.1.call-start = ((), (), s32[]{:S(2)}) async-start(), calls=%async_computation.3 | async-start | bytes 3538944 | tf_op jit(solution)/shard_map/all_gather | solution.py:30
  152.7 4.9 %copy-start.1 = (bf16[1,128,768]{2,1,0:T(8,128)(2,1)S(1)}, bf16[1,128,768]{2,1,0:T(8,128)(2,1)}, u32[]{:S(2)}) copy-start(bf16[1,128,768]{2,1,0:T(8,128)(2,1)} %param.16) | copy-start | bytes 589828
  152.7 5.6 %copy-start.2 = (f32[768]{0:T(1024)S(1)}, f32[768]{0:T(1024)}, u32[]{:S(2)}) copy-start(f32[768]{0:T(1024)} %param.24) | copy-start | bytes 9220
  157.6 7.9 %copy-start.5 = (s32[1,128]{1,0:T(1,128)S(1)}, s32[1,128]{1,0:T(1,128)}, u32[]{:S(2)}) copy-start(s32[1,128]{1,0:T(1,128)} %param.20) | copy-start | bytes 1540
  270.7 16.9 %copy-start.3 = (s32[16]{0:T(128)S(1)}, s32[16]{0:T(128)}, u32[]{:S(2)}) copy-start(s32[16]{0:T(128)} %param.21) | copy-start | bytes 196
  271.5 15.9 %all-to-all-start = ((f32[16,48,128]{2,1,0:T(8,128)}), f32[16,48,128]{2,1,0:T(8,128)S(1)}, u32[]{:S(2)}, u32[]{:S(2)}) async-start(f32[16,48,128]{2,1,0:T(8,128)} %broadcast_in_dim.91), calls=%async_computation | async-start | bytes 786432 | tf_op jit(solution)/shard_map/all_to_all | solution.py:43
  288.4 20.9 %all-to-all-start.1 = ((f32[32,1,16]{2,1,0:T(1,128)}), f32[32,1,16]{2,1,0:T(1,128)S(1)}, u32[]{:S(2)}, u32[]{:S(2)}) async-start(f32[32,1,16]{2,1,0:T(1,128)} %broadcast_in_dim.93), calls=%async_computation.1 | async-start | bytes 32768 | tf_op jit(solution)/shard_map/all_to_all | solution.py:43
  310.0 5.8 %copy-start.4 = (f32[16]{0:T(128)}, f32[16]{0:T(128)S(1)}, u32[]{:S(2)}) copy-start(f32[16]{0:T(128)S(1)} %get-tuple-element.352) | copy-start | bytes 196
Sparse Core Ops, SparseCore 0:
  11.9 140.7 all-gather.7
  165.6 75.8 all-gather.9
where the time goes:
time: 323 us
  waiting for transfers between devices  219 us (68%)
  blocking collectives  23.5 us (7%)
  between operations  17.7 us (5%)
  matrix products  17 us (5%)
  starting transfers between devices  16.5 us (5%)
  local copies, waits for them, and re-layouts  13.8 us (4%)
  other arithmetic  11.6 us (4%)
    all_gather x1, waiting for transfers between devices, shards(): shard_piece = lax.all_gather(key_value, 'seq', axis=1, tiled=True)  141 us
    all_gather x1, waiting for transfers between devices, all_blocks(): blocks = lax.all_gather(blocks, axes[k], axis=0, tiled=True)  59.3 us
    all_gather x3, blocking collectives, all_blocks(): blocks = lax.all_gather(blocks, axes[k], axis=0, tiled=True)  23.5 us
    all_to_all x2, waiting for transfers between devices, from_everyone(): return lax.all_to_all(copies, axis, split_axis=0, concat_axis=0, tiled=True)  19.3 us
    all_to_all x2, starting transfers between devices, from_everyone(): return lax.all_to_all(copies, axis, split_axis=0, concat_axis=0, tiled=True)  16.4 us
    dot_general x4, matrix products, shard_stats(): logits = jnp.dot(block, unembed, preferred_element_type=jnp.float32)  14.6 us
  transfers between devices with their start and end apart: 4, of which 4 were waited for; matrix products, arithmetic and copies ran while one was open for 0% of the time, Pallas kernels for 0%

commit v1 on v0

v1 whole, which is shorter than its diff:
```python
import math

import jax
import jax.numpy as jnp
from jax import lax
from jax.experimental import pallas as pl
from jax.experimental.pallas import tpu as pltpu
from jax.sharding import Mesh
from jax.sharding import PartitionSpec as P

HEADS = 12
HEAD_DIM = 64
ROT = 16
D = 768
ROWS = 128
SHARE = 1664
WIDE = 2 * SHARE
TILE = 256
TILES = WIDE // TILE
DOCS = 16
SEQ = 32
CHUNK = 512
NEGATIVE = -1e30
ROTARY_BASE = 10000.0
NORM_EPSILON = 1e-05
SPREAD_EPSILON = 0.0001
LOG2E = 1.4426950408889634
MESH = pl.DeviceIdType.MESH
F32 = jnp.float32
BF16 = jnp.bfloat16


def lanes(shape):
    return lax.broadcasted_iota(jnp.int32, shape, len(shape) - 1)


def rows_of(shape):
    return lax.broadcasted_iota(jnp.int32, shape, len(shape) - 2)


def rcopy(src, dst, ss, rs, **where):
    return pltpu.make_async_remote_copy(
        src_ref=src,
        dst_ref=dst,
        send_sem=ss,
        recv_sem=rs,
        device_id=where,
        device_id_type=MESH,
    )


def kernel(
    lengths_ref,
    rank_ref,
    q_ref,
    k_ref,
    v_ref,
    hid_ref,
    cos_ref,
    sin_ref,
    tgt_ref,
    gain_ref,
    ow_ref,
    un_ref,
    nll_ref,
    ppl_ref,
    acc_out_ref,
    packed,
    got,
    outs,
    att,
    attended,
    qt,
    s_scr,
    mx_ref,
    sum_ref,
    pv_ref,
    wide,
    rows_buf,
    relay,
    logit,
    tgts,
    stat_out,
    stats,
    seqs,
    docs,
    a_send,
    a_recv,
    f_send,
    f_recv,
    r_send,
    r_recv,
    w_sem,
    c_send,
    c_recv,
    t_send,
    t_recv,
    s_send,
    s_recv,
    q_send,
    q_recv,
    d_send,
    d_recv,
):
    xh = lax.axis_index("xh")
    y = lax.axis_index("y")
    c = lax.axis_index("c")
    xl = lax.axis_index("xl")
    z = lax.axis_index("z")
    me = xh * 8 + y
    seq = me * 2 + c
    doc = xl * 8 + z
    sig = 1 - 2 * lax.rem(z, 2)
    z_up = lax.rem(z + sig + 8, 8)
    z_dn = lax.rem(z - sig + 8, 8)
    z_pair = z + sig

    barrier = pltpu.get_barrier_semaphore()

    def greet_seq(n, carry):
        @pl.when(n != seq)
        def _():
            pl.semaphore_signal(
                barrier,
                inc=1,
                device_id={"xh": n // 16, "y": lax.rem(n // 2, 8), "c": lax.rem(n, 2)},
                device_id_type=MESH,
            )

        return carry

    def greet_doc(n, carry):
        @pl.when(n != doc)
        def _():
            pl.semaphore_signal(
                barrier,
                inc=1,
                device_id={"xl": n // 8, "z": lax.rem(n, 8)},
                device_id_type=MESH,
            )

        return carry

    lax.fori_loop(0, SEQ, greet_seq, 0)
    lax.fori_loop(0, DOCS, greet_doc, 0)

    mine = pltpu.make_async_copy(un_ref, wide.at[:, pl.ds(0, SHARE)], w_sem.at[4])
    mine.start()

    lane = lanes((ROWS, ROWS))
    low = lane < HEAD_DIM
    first = lax.rem(lane, HEAD_DIM) < ROT // 2
    cosine = cos_ref[...]
    sine = sin_ref[...]
    low_half = low[:HEAD_DIM]

    def turn(block):
        partner = jnp.where(first, pltpu.roll(block, ROWS - 8, 1), pltpu.roll(block, 8, 1))
        return block * cosine + partner * sine

    for pair in range(HEADS // 2):
        at = slice(pair * ROWS, (pair + 1) * ROWS)
        tk = turn(k_ref[:, at].astype(F32))
        tq = turn(q_ref[:, at].astype(F32))
        tv = v_ref[:, at].astype(F32)
        rk = pltpu.roll(tk, HEAD_DIM, 1)
        rq = pltpu.roll(tq, HEAD_DIM, 1)
        rv = pltpu.roll(tv, HEAD_DIM, 1)
        packed[2 * pair, 0:ROWS] = jnp.where(low, tk, rv).astype(BF16)
        packed[2 * pair + 1, 0:ROWS] = jnp.where(low, rk, tv).astype(BF16)
        packed[2 * pair, ROWS : ROWS + HEAD_DIM] = jnp.where(
            low_half, tq[:HEAD_DIM], rq[HEAD_DIM:]
        ).astype(BF16)
        packed[2 * pair + 1, ROWS : ROWS + HEAD_DIM] = jnp.where(
            low_half, rq[:HEAD_DIM], tq[HEAD_DIM:]
        ).astype(BF16)

    pl.semaphore_wait(barrier, SEQ - 1 + DOCS - 1)

    is_head = jnp.logical_and(y != 3, y != 7)
    my_slot = y - jnp.where(y > 3, 1, 0)
    my_head = jnp.where(is_head, xh * 6 + my_slot, -1)

    def head_copy(h):
        yi = lax.rem(h, 6)
        return rcopy(
            packed.at[h],
            got.at[seq],
            a_send.at[h],
            a_recv.at[me],
            xh=h // 6,
            y=yi + jnp.where(yi > 2, 1, 0),
        )

    def send_head(n, carry):
        h = lax.rem(n + me, HEADS)

        @pl.when(h != my_head)
        def _():
            head_copy(h).start()

        @pl.when(h == my_head)
        def _():
            got[seq] = packed[h]

        return carry

    lax.fori_loop(0, HEADS, send_head, 0)

    half_rows = pl.ds(pl.multiple_of(c * (D // 2), D // 2), D // 2)
    swap = rcopy(
        un_ref.at[half_rows],
        wide.at[half_rows, pl.ds(SHARE, SHARE)],
        w_sem.at[0],
        w_sem.at[1],
        z=z_pair,
    )
    swap.start()

    def target_copy(n):
        side = n // 4
        step = lax.rem(n, 4)
        move = jnp.where(
            step == 0, 0, jnp.where(step == 1, -sig, jnp.where(step == 2, 2 * sig, -3 * sig))
        )
        return rcopy(
            tgt_ref,
            tgts.at[n],
            t_send.at[n],
            t_recv.at[n],
            xl=lax.rem(xl + side, 2),
            z=lax.rem(z + move + 8, 8),
        )

    tgts[0] = tgt_ref[...]

    def send_target(n, carry):
        target_copy(n).start()
        return carry

    lax.fori_loop(1, 8, send_target, 0)

    def arrival(i):
        @pl.when(i != me)
        def _():
            rcopy(
                packed.at[0], got.at[2 * i + c], a_send.at[0], a_recv.at[i], xh=xh, y=y
            ).wait_recv()

        forward(i).start()

    def forward(i):
        piece = got.at[2 * i + c, pl.ds(0, ROWS)]
        return rcopy(piece, piece, f_send.at[i], f_recv.at[i], c=1 - c)

    def forwarded(i):
        piece = got.at[2 * i + 1 - c, pl.ds(0, ROWS)]
        return rcopy(piece, piece, f_send.at[i], f_recv.at[i], c=1 - c)

    scale = LOG2E / math.sqrt(HEAD_DIM)

    def result_copy(i):
        return rcopy(
            outs.at[i],
            att.at[my_head],
            r_send.at[i],
            r_recv.at[my_head],
            xh=i // 8,
            y=lax.rem(i, 8),
        )

    def query_step(t, carry):
        @pl.when(t < 7)
        def _():
            arrival(2 * t + 2)
            arrival(2 * t + 3)

        for u in range(2):
            qp = got[4 * t + 2 * u + c, ROWS : ROWS + HEAD_DIM].astype(F32)
            qt[u * ROWS : u * ROWS + HEAD_DIM] = jnp.where(low_half, qp, 0.0).astype(BF16)
            qt[u * ROWS + HEAD_DIM : (u + 1) * ROWS] = jnp.where(
                low_half, pltpu.roll(qp, HEAD_DIM, 1), 0.0
            ).astype(BF16)
        mx_ref[...] = jnp.full((2 * ROWS, ROWS), NEGATIVE, F32)
        sum_ref[...] = jnp.zeros((2 * ROWS, ROWS), F32)
        pv_ref[...] = jnp.zeros((2 * ROWS, ROWS), F32)
        forwarded(2 * t).wait_recv()
        forwarded(2 * t + 1).wait_recv()

        def scores(j, masked):
            block = got[pl.ds(4 * j, 4), 0:ROWS].reshape(CHUNK, ROWS)
            s = lax.dot_general(
                qt[...], block, (((1,), (1,)), ((), ())), preferred_element_type=F32
            )
            if masked:
                shape = (2 * ROWS, CHUNK)
                row = rows_of(shape)
                place = row + jnp.where(row >= ROWS, ROWS, 0) + c * ROWS
                s = jnp.where(lanes(shape) <= place, s, NEGATIVE)
            s_scr[j] = s
            top = mx_ref[...]
            for g in range(CHUNK // ROWS):
                top = jnp.maximum(top, s[:, g * ROWS : (g + 1) * ROWS])
            mx_ref[...] = top

        def plain(j, inner):
            scores(j, False)
            return inner

        lax.fori_loop(0, t, plain, 0)
        scores(t, True)
        top = jnp.max(mx_ref[...], axis=1, keepdims=True) * scale

        def weigh(j, inner):
            block = got[pl.ds(4 * j, 4), 0:ROWS].reshape(CHUNK, ROWS)
            p = jnp.exp2(s_scr[j] * scale - top)
            total = sum_ref[...]
            for g in range(CHUNK // ROWS):
                total = total + p[:, g * ROWS : (g + 1) * ROWS]
            sum_ref[...] = total
            pv_ref[...] += jnp.dot(p.astype(BF16), block, preferred_element_type=F32)
            return inner

        lax.fori_loop(0, t + 1, weigh, 0)
        out = pv_ref[...] / jnp.sum(sum_ref[...], axis=1, keepdims=True)
        for u in range(2):
            i = 2 * t + u
            top_part = out[u * ROWS : u * ROWS + HEAD_DIM]
            bottom = out[u * ROWS + HEAD_DIM : (u + 1) * ROWS]
            whole = jnp.where(low_half, pltpu.roll(top_part, HEAD_DIM, 1), bottom).astype(BF16)
            outs[i] = whole

            @pl.when(i != me)
            def _():
                result_copy(i).start()

            @pl.when(i == me)
            def _():
                att[my_head] = whole

        return carry

    @pl.when(is_head)
    def _():
        arrival(0)
        arrival(1)
        lax.fori_loop(0, 8, query_step, 0)

    swap.wait_recv()
    share = wide.at[half_rows, pl.ds(SHARE, SHARE)]
    pass_on = rcopy(share, share, w_sem.at[2], w_sem.at[3], c=1 - c)
    pass_on.start()

    def wait_result(h, carry):
        @pl.when(h != my_head)
        def _():
            rcopy(outs.at[0], att.at[h], r_send.at[0], r_recv.at[h], xh=xh, y=y).wait_recv()

        return carry

    lax.fori_loop(0, HEADS, wait_result, 0)
    for pair in range(HEADS // 2):
        at = slice(pair * ROWS, (pair + 1) * ROWS)
        even = att[2 * pair].astype(F32)
        odd = att[2 * pair + 1].astype(F32)
        attended[0:HEAD_DIM, at] = jnp.where(
            low_half, even, pltpu.roll(odd, HEAD_DIM, 1)
        ).astype(BF16)
        attended[HEAD_DIM:ROWS, at] = jnp.where(
            low_half, pltpu.roll(even, HEAD_DIM, 1), odd
        ).astype(BF16)
    residual = hid_ref[...].astype(F32) + jnp.dot(
        attended[...], ow_ref[...], preferred_element_type=F32
    )
    center = residual - jnp.sum(residual, axis=1, keepdims=True) * (1.0 / D)
    spread = jnp.sum(center * center, axis=1, keepdims=True) * (1.0 / D)
    rows_buf[0] = (center * lax.rsqrt(spread + NORM_EPSILON) * gain_ref[...]).astype(BF16)

    def row_copy(n):
        if n < 4:
            return rcopy(
                rows_buf.at[n], rows_buf.at[4 + n], c_send.at[n], c_recv.at[4 + n], xl=1 - xl
            )
        if n == 4:
            return rcopy(rows_buf.at[0], rows_buf.at[1], c_send.at[4], c_recv.at[1], z=z_dn)
        if n == 5:
            return rcopy(rows_buf.at[0], relay.at[0], c_send.at[5], c_recv.at[8], z=z_up)
        if n == 6:
            return rcopy(rows_buf.at[1], relay.at[1], c_send.at[6], c_recv.at[9], z=z_up)
        if n == 7:
            return rcopy(relay.at[0], rows_buf.at[2], c_send.at[7], c_recv.at[2], z=z_dn)
        return rcopy(relay.at[1], rows_buf.at[3], c_send.at[8], c_recv.at[3], z=z_dn)

    def row_wait(slot):
        ref = relay.at[slot - 8] if slot >= 8 else rows_buf.at[slot]
        rcopy(rows_buf.at[0], ref, c_send.at[0], c_recv.at[slot], z=z_dn).wait_recv()

    row_copy(4).start()
    row_copy(5).start()
    row_copy(0).start()
    mine.wait()
    pass_on.wait_recv()

    def wait_target(n, carry):
        rcopy(tgt_ref, tgts.at[n], t_send.at[n], t_recv.at[n], z=z_dn).wait_recv()
        return carry

    lax.fori_loop(1, 8, wait_target, 0)
    diagonal = lane == rows_of((ROWS, ROWS))
    other = xl * 8 + z_pair

    def stat_copy(slot):
        side = slot // 4
        back = lax.rem(z - sig * lax.rem(slot, 4) + 8, 8)
        return rcopy(
            stat_out.at[slot],
            stats.at[xl * 4 + z // 2],
            s_send.at[slot],
            s_recv.at[xl * 4 + z // 2],
            xl=lax.rem(xl + side, 2),
            z=back,
        )

    def as_row(column):
        return jnp.sum(jnp.where(diagonal, column, 0.0), axis=0, keepdims=True)

    def score_rows(n, carry):
        slot = lax.rem(n, 2) * 4 + n // 2

        @pl.when(n == 1)
        def _():
            row_wait(1)
            row_copy(6).start()
            row_copy(1).start()
            row_wait(8)
            row_copy(7).start()
            row_wait(4)

        @pl.when(n == 2)
        def _():
            row_wait(9)
            row_copy(8).start()
            row_wait(2)
            row_copy(2).start()

        @pl.when(n == 3)
        def _():
            row_wait(5)

        @pl.when(n == 4)
        def _():
            row_wait(3)
            row_copy(3).start()

        @pl.when(n == 5)
        def _():
            row_wait(6)

        @pl.when(n == 7)
        def _():
            row_wait(7)

        block = rows_buf[slot]
        mx_ref[0:ROWS] = jnp.full((ROWS, ROWS), NEGATIVE, F32)

        def multiply(k, inner):
            s = jnp.dot(
                block,
                wide[:, pl.ds(pl.multiple_of(k * TILE, TILE), TILE)],
                preferred_element_type=F32,
            )
            logit[k] = s
            mx_ref[0:ROWS] = jnp.maximum(
                mx_ref[0:ROWS], jnp.maximum(s[:, :ROWS], s[:, ROWS:])
            )
            return inner

        lax.fori_loop(0, TILES, multiply, 0)
        wanted = jnp.sum(jnp.where(diagonal, tgts[slot], 0.0), axis=1, keepdims=True)
        wanted = wanted.astype(jnp.int32)
        here = wanted - doc * SHARE
        there = wanted - other * SHARE
        place = jnp.where(
            jnp.logical_and(here >= 0, here < SHARE),
            here,
            jnp.where(jnp.logical_and(there >= 0, there < SHARE), there + SHARE, -1),
        )
        place = jnp.broadcast_to(place, (ROWS, ROWS)) - lane
        top = jnp.max(mx_ref[0:ROWS], axis=1, keepdims=True)
        top2 = jnp.broadcast_to(top * LOG2E, (ROWS, ROWS))
        sum_ref[0:ROWS] = jnp.zeros((ROWS, ROWS), F32)
        pv_ref[0:ROWS] = jnp.zeros((ROWS, ROWS), F32)

        def add_up(k, inner):
            total = sum_ref[0:ROWS]
            pick = pv_ref[0:ROWS]
            for g in range(TILE // ROWS):
                s = logit[k, :, g * ROWS : (g + 1) * ROWS]
                total = total + jnp.exp2(s * LOG2E - top2)
                pick = pick + jnp.where(place == k * TILE + g * ROWS, s, 0.0)
            sum_ref[0:ROWS] = total
            pv_ref[0:ROWS] = pick
            return inner

        lax.fori_loop(0, TILES, add_up, 0)
        lse = top + jnp.log(jnp.sum(sum_ref[0:ROWS], axis=1, keepdims=True))
        pick = jnp.sum(pv_ref[0:ROWS], axis=1, keepdims=True)
        row8 = rows_of((8, ROWS))
        tile = jnp.where(row8 == 0, as_row(lse), as_row(pick))

        @pl.when(n != 0)
        def _():
            stat_out[slot] = tile
            stat_copy(slot).start()

        @pl.when(n == 0)
        def _():
            stats[xl * 4 + z // 2] = tile

        return carry

    lax.fori_loop(0, 8, score_rows, 0)

    def wait_stat(n, carry):
        @pl.when(n != xl * 4 + z // 2)
        def _():
            rcopy(stat_out.at[0], stats.at[n], s_send.at[0], s_recv.at[n], z=z_dn).wait_recv()

        return carry

    lax.fori_loop(0, 8, wait_stat, 0)
    parts = [stats[n] for n in range(8)]
    top = parts[0][0:1]
    for part in parts[1:]:
        top = jnp.maximum(top, part[0:1])
    total = jnp.zeros((1, ROWS), F32)
    pick = jnp.zeros((1, ROWS), F32)
    for part in parts:
        total = total + jnp.exp(part[0:1] - top)
        pick = pick + part[1:2]
    place = seq * ROWS + lanes((1, ROWS))
    nll = jnp.where(place < lengths_ref[doc], top + jnp.log(total) - pick, 0.0)
    nll_ref[...] = nll
    seqs[seq] = jnp.broadcast_to(jnp.sum(nll, axis=1, keepdims=True), (1, ROWS))

    def seq_copy(n):
        return rcopy(
            seqs.at[seq],
            seqs.at[seq],
            q_send.at[n],
            q_recv.at[seq],
            xh=n // 16,
            y=lax.rem(n // 2, 8),
            c=lax.rem(n, 2),
        )

    def send_seq(n, carry):
        @pl.when(n != seq)
        def _():
            seq_copy(n).start()

        return carry

    def wait_seq(n, carry):
        @pl.when(n != seq)
        def _():
            rcopy(seqs.at[n], seqs.at[n], q_send.at[n], q_recv.at[n], xh=xh, y=y, c=c).wait_recv()

        return carry

    lax.fori_loop(0, SEQ, send_seq, 0)
    lax.fori_loop(0, SEQ, wait_seq, 0)
    docs[doc] = jnp.sum(seqs[...], axis=0)

    def doc_copy(n):
        return rcopy(
            docs.at[doc],
            docs.at[doc],
            d_send.at[n],
            d_recv.at[doc],
            xl=n // 8,
            z=lax.rem(n, 8),
        )

    def send_doc(n, carry):
        @pl.when(n != doc)
        def _():
            doc_copy(n).start()

        return carry

    def wait_doc(n, carry):
        @pl.when(n != doc)
        def _():
            rcopy(docs.at[n], docs.at[n], d_send.at[n], d_recv.at[n], xl=xl, z=z).wait_recv()

        return carry

    lax.fori_loop(0, DOCS, send_doc, 0)
    lax.fori_loop(0, DOCS, wait_doc, 0)

    shape = (DOCS, ROWS)
    row = rows_of(shape)
    col = lanes(shape)
    column = docs[...].reshape(DOCS, ROWS)
    for d in range(DOCS):
        column = jnp.where(row == d, column / lengths_ref[d].astype(F32), column)
    valid = lanes((1, ROWS)) < DOCS
    line = jnp.sum(jnp.where(row == col, column, 0.0), axis=0, keepdims=True)
    mean = jnp.sum(line, axis=1, keepdims=True) * (1.0 / DOCS)
    off = jnp.where(valid, line - mean, 0.0)
    spread = jnp.sqrt(jnp.sum(off * off, axis=1, keepdims=True) * (1.0 / DOCS) + SPREAD_EPSILON)
    ahead = jnp.logical_or(
        column < line, jnp.logical_and(column == line, row < col)
    )
    rank = jnp.sum(jnp.where(ahead, 1.0, 0.0), axis=0, keepdims=True)
    scaled = rank_ref[0] * (DOCS - 1)
    low_index = lax.div(scaled, 99)
    high_index = jnp.minimum(low_index + 1, DOCS - 1)
    fraction = (scaled - 99 * low_index).astype(F32) / 99.0
    hit_low = jnp.logical_and(valid, rank == low_index.astype(F32))
    hit_high = jnp.logical_and(valid, rank == high_index.astype(F32))
    low_value = jnp.sum(jnp.where(hit_low, line, 0.0), axis=1, keepdims=True)
    high_value = jnp.sum(jnp.where(hit_high, line, 0.0), axis=1, keepdims=True)
    level = (1.0 - fraction) * low_value + fraction * high_value
    ppl_ref[...] = line
    acc_out_ref[...] = jax.nn.sigmoid((level - line) / spread)

    def drain_head(h, carry):
        @pl.when(h != my_head)
        def _():
            head_copy(h).wait_send()

        return carry

    lax.fori_loop(0, HEADS, drain_head, 0)

    def drain_work(i, carry):
        forward(i).wait_send()

        @pl.when(i != me)
        def _():
            result_copy(i).wait_send()

        return carry

    @pl.when(is_head)
    def _():
        lax.fori_loop(0, 16, drain_work, 0)

    swap.wait_send()
    pass_on.wait_send()
    for n in range(9):
        row_copy(n).wait_send()

    def drain_small(n, carry):
        target_copy(n).wait_send()
        stat_copy(n).wait_send()
        return carry

    lax.fori_loop(1, 8, drain_small, 0)

    def drain_seq(n, carry):
        @pl.when(n != seq)
        def _():
            seq_copy(n).wait_send()

        return carry

    def drain_doc(n, carry):
        @pl.when(n != doc)
        def _():
            doc_copy(n).wait_send()

        return carry

    lax.fori_loop(0, SEQ, drain_seq, 0)
    lax.fori_loop(0, DOCS, drain_doc, 0)


def shards(
    hidden,
    queries,
    key_states,
    values,
    targets,
    lengths,
    keep_rank,
    out_weight,
    final_gain,
    unembed,
):
    seq = lax.axis_index("xh") * 16 + lax.axis_index("y") * 2 + lax.axis_index("c")
    place = (seq * ROWS + jnp.arange(ROWS, dtype=jnp.int32)).astype(F32)
    spot = jnp.arange(ROWS, dtype=jnp.int32) % HEAD_DIM
    turn = (spot % (ROT // 2)).astype(F32)
    inv_freq = ROTARY_BASE ** (-2.0 * turn / ROT)
    angles = place[:, None] * inv_freq[None, :]
    cosine = jnp.where(spot < ROT, jnp.cos(angles), 1.0)
    sine = jnp.sin(angles)
    sine = jnp.where(spot < ROT // 2, -sine, jnp.where(spot < ROT, sine, 0.0))
    vmem = pl.BlockSpec(memory_space=pltpu.VMEM)
    smem = pl.BlockSpec(memory_space=pltpu.SMEM)
    dma = pltpu.SemaphoreType.DMA
    nll, ppl, acceptance = pl.pallas_call(
        kernel,
        name="scoring",
        out_shape=(
            jax.ShapeDtypeStruct((1, ROWS), F32),
            jax.ShapeDtypeStruct((1, ROWS), F32),
            jax.ShapeDtypeStruct((1, ROWS), F32),
        ),
        in_specs=[smem, smem] + [vmem] * 9 + [pl.BlockSpec(memory_space=pl.ANY)],
        out_specs=(vmem, vmem, vmem),
        scratch_shapes=[
            pltpu.VMEM((HEADS, ROWS + HEAD_DIM, ROWS), BF16),
            pltpu.VMEM((SEQ, ROWS + HEAD_DIM, ROWS), BF16),
            pltpu.VMEM((16, HEAD_DIM, ROWS), BF16),
            pltpu.VMEM((HEADS, HEAD_DIM, ROWS), BF16),
            pltpu.VMEM((ROWS, D), BF16),
            pltpu.VMEM((2 * ROWS, ROWS), BF16),
            pltpu.VMEM((8, 2 * ROWS, CHUNK), F32),
            pltpu.VMEM((2 * ROWS, ROWS), F32),
            pltpu.VMEM((2 * ROWS, ROWS), F32),
            pltpu.VMEM((2 * ROWS, ROWS), F32),
            pltpu.VMEM((D, WIDE), BF16),
            pltpu.VMEM((8, ROWS, D), BF16),
            pltpu.VMEM((2, ROWS, D), BF16),
            pltpu.VMEM((TILES, ROWS, TILE), F32),
            pltpu.VMEM((8, 1, ROWS), F32),
            pltpu.VMEM((8, 8, ROWS), F32),
            pltpu.VMEM((8, 8, ROWS), F32),
            pltpu.VMEM((SEQ, 1, ROWS), F32),
            pltpu.VMEM((DOCS, 1, ROWS), F32),
            dma((HEADS,)),
            dma((16,)),
            dma((16,)),
            dma((16,)),
            dma((16,)),
            dma((HEADS,)),
            dma((5,)),
            dma((9,)),
            dma((10,)),
            dma((8,)),
            dma((8,)),
            dma((8,)),
            dma((8,)),
            dma((SEQ,)),
            dma((SEQ,)),
            dma((DOCS,)),
            dma((DOCS,)),
        ],
        compiler_params=pltpu.CompilerParams(
            collective_id=0, has_side_effects=True, vmem_limit_bytes=48 * 1024 * 1024
        ),
    )(
        lengths,
        keep_rank,
        queries[0],
        key_states[0],
        values[0],
        hidden[0],
        cosine,
        sine,
        targets.astype(F32),
        final_gain[None, :],
        out_weight,
        unembed,
    )
    return (nll, ppl[0, :DOCS], acceptance[0, :DOCS])


def solution(mesh):
    split = Mesh(mesh.devices.reshape(2, 8, 2, 2, 8), ("xh", "y", "c", "xl", "z"))
    rows = ("xh", "y", "c")
    parts = ("xl", "z")
    placed = (
        P(parts, rows, None),
        P(parts, rows, None),
        P(parts, rows, None),
        P(parts, rows, None),
        P(parts, rows),
        P(),
        P(),
        P(),
        P(),
        P(None, parts),
    )
    return jax.shard_map(
        shards, mesh=split, in_specs=placed, out_specs=(P(parts, rows), P(), P()), check_vma=False
    )
```

time: 323 us -> 125 us (0.39)
  waiting for transfers between devices: 219 us -> 0 us
  Pallas kernels: 0 us -> 112 us
  blocking collectives: 23.5 us -> 0 us
  matrix products: 17 us -> 0 us
  starting transfers between devices: 16.5 us -> 0 us
  between operations: 17.7 us -> 1.34 us
  other arithmetic: 11.6 us -> 0.99 us
  local copies, waits for them, and re-layouts: 13.8 us -> 9.57 us
    all_gather x2 -> x0, waiting for transfers between devices: 200 us -> none  [the longest x1 141 us: shards(): shard_piece = lax.all_gather(key_value, 'seq', axis=1, tiled=True)]
    pallas_call x0 -> x1, Pallas kernels: none -> 112 us  [shards(): pl.pallas_call(kernel, name='scoring', out_shape=(jax.ShapeDtypeStruct((1...]
    all_gather x3 -> x0, blocking collectives: 23.5 us -> none  [all_blocks(): blocks = lax.all_gather(blocks, axes[k], axis=0, tiled=True)]
    all_to_all x2 -> x0, waiting for transfers between devices: 19.3 us -> none  [from_everyone(): return lax.all_to_all(copies, axis, split_axis=0, concat_axis=0, tiled=True)]
    dot_general x7 -> x0, matrix products: 17 us -> none  [the longest x4 14.6 us: shard_stats(): logits = jnp.dot(block, unembed, preferred_element_type=jnp.float32)]
    all_to_all x2 -> x0, starting transfers between devices: 16.4 us -> none  [from_everyone(): return lax.all_to_all(copies, axis, split_axis=0, concat_axis=0, tiled=True)]
    reduce_sum x11 -> x0, other arithmetic: 7.85 us -> none  [the longest x4 4.8 us: shard_stats(): picked = jnp.sum(jnp.where(matches, logits, 0.0), axis=1)]
    unnamed x15, local copies, waits for them, and re-layouts: 3.38 us -> 7.86 us
  transfers between devices with their start and end apart: 4 -> 0, of which waited for: 4 -> 0; matrix products, arithmetic and copies ran while one was open for 0% -> 0% of each run, Pallas kernels for 0% -> 0%
where the time goes in v1:
time: 125 us; the launch traced here: 124 us
  Pallas kernels  112 us (90%)
  local copies, waits for them, and re-layouts  9.57 us (8%)
  between operations  1.34 us (1%)
    pallas_call x1, Pallas kernels, shards(): pl.pallas_call(kernel, name='scoring', out_shape=(jax.ShapeDtypeStruct((1...  112 us
    unnamed x15, local copies, waits for them, and re-layouts  7.86 us

profile of v1, /device:TPU:1, one launch (start us, length us, event | category | flops | bytes accessed | tf_op | source)
XLA Modules:
  0.0 124.1 jit_solution(12972320930382398203)
XLA Ops:
  0.7 0.3 fusion.2
  1.0 0.7 broadcast_in_dim.27.gain_ref
  1.7 0.7 convert_element_type.19.tgt_ref
  3.0 0.0 copy-start
  3.0 1.7 %copy-done = bf16[768,1664]{1,0:T(8,128)(2,1)S(1)} copy-done((bf16[768,1664]{1,0:T(8,128)(2,1)S(1)}, bf16[768,1664]{1,0:T(8,128)(2,1)}, u32[]{:S(2)}) %copy-start) | copy-done | bytes 2555928
  4.7 0.0 copy-start.1
  4.7 1.3 %copy-done.1 = bf16[768,768]{1,0:T(8,128)(2,1)S(1)} copy-done((bf16[768,768]{1,0:T(8,128)(2,1)S(1)}, bf16[768,768]{1,0:T(8,128)(2,1)}, u32[]{:S(2)}) %copy-start.1) | copy-done | bytes 1179672
  6.0 0.0 copy-start.2
  6.0 0.9 copy-done.2
  6.9 0.0 copy-start.3
  6.9 0.9 copy-done.3
  7.9 0.0 copy-start.4
  7.9 0.9 copy-done.4
  8.8 0.0 copy-start.5
  8.8 0.9 copy-done.5
  9.7 0.0 copy-start.6
  9.7 0.7 copy-done.6
  10.4 112.2 %scoring.1 = (f32[1,128]{1,0:T(1,128)S(1)}, f32[1,128]{1,0:T(1,128)S(1)}, f32[1,128]{1,0:T(1,128)S(1)}) custom-call(s32[16]{0:T(128)S(1)} %copy-done.6, s32[1]{0:T(128)S(6)} %copy.14.rank_ref, bf16[128,768]{1,0:T(8,128)(2,1)S(1)} %bitcast.8, bf16[128,768]{1,0:T(8,128)(2,1)S(1)} %bitcast.9, bf16[128,768]{1,0:T(8,128)(2,1)S(1)} %bitcast.10, ...), custom_call_target="tpu_custom_call" | custom-call | tf_op jit(solution)/shard_map/scoring/pallas_call | solution.py:705
  122.6 0.5 slice_bitcast_fusion
  123.1 0.5 slice_bitcast_fusion.1
  123.6 0.5 copy.15
  (3 shorter events, 0.0 us)
Async XLA Ops:
  3.0 1.7 %copy-start = (bf16[768,1664]{1,0:T(8,128)(2,1)S(1)}, bf16[768,1664]{1,0:T(8,128)(2,1)}, u32[]{:S(2)}) copy-start(bf16[768,1664]{1,0:T(8,128)(2,1)} %un_ref.1) | copy-start | bytes 7667716
  4.7 1.3 %copy-start.1 = (bf16[768,768]{1,0:T(8,128)(2,1)S(1)}, bf16[768,768]{1,0:T(8,128)(2,1)}, u32[]{:S(2)}) copy-start(bf16[768,768]{1,0:T(8,128)(2,1)} %ow_ref.1) | copy-start | bytes 3538948
  6.0 0.9 copy-start.2
  6.9 0.9 copy-start.3
  7.9 0.9 copy-start.4
  8.8 0.9 copy-start.5
  9.7 0.7 copy-start.6

commit v2 on v1

v2 whole, which is shorter than its diff:
```python
import math

import jax
import jax.numpy as jnp
import numpy as np
from jax import lax
from jax.experimental import pallas as pl
from jax.experimental.pallas import tpu as pltpu
from jax.sharding import Mesh
from jax.sharding import PartitionSpec as P

HEADS = 12
HEAD_DIM = 64
ROT = 16
D = 768
ROWS = 128
SHARE = 1664
WIDE = 2 * SHARE
TILE = 256
TILES = WIDE // TILE
DOCS = 16
SEQ = 32
CHUNK = 1024
SPAN = 512
NEGATIVE = -1e30
ROTARY_BASE = 10000.0
NORM_EPSILON = 1e-05
SPREAD_EPSILON = 0.0001
LOG2E = 1.4426950408889634
MESH = pl.DeviceIdType.MESH
F32 = jnp.float32
BF16 = jnp.bfloat16


def lanes(shape):
    return lax.broadcasted_iota(jnp.int32, shape, len(shape) - 1)


def rows_of(shape):
    return lax.broadcasted_iota(jnp.int32, shape, len(shape) - 2)


def rcopy(src, dst, ss, rs, **where):
    return pltpu.make_async_remote_copy(
        src_ref=src,
        dst_ref=dst,
        send_sem=ss,
        recv_sem=rs,
        device_id=where,
        device_id_type=MESH,
    )


def kernel(
    base_in,
    step_in,
    lengths_in,
    rank_in,
    q_in,
    k_in,
    v_in,
    hid_in,
    tgt_ref,
    gain_in,
    ow_in,
    un_ref,
    final_ref,
    base_ref,
    step_ref,
    lengths_ref,
    rank_ref,
    q_ref,
    k_ref,
    v_ref,
    hid_ref,
    gain_ref,
    ow_ref,
    packed,
    got,
    outs,
    att,
    attended,
    qt,
    s_scr,
    mx_ref,
    sum_ref,
    pv_ref,
    wide,
    rows_buf,
    relay,
    logit,
    tgts,
    stat_out,
    stats,
    seqs,
    docs,
    a_send,
    a_recv,
    f_send,
    f_recv,
    r_send,
    r_recv,
    w_sem,
    c_send,
    c_recv,
    t_send,
    t_recv,
    s_send,
    s_recv,
    q_send,
    q_recv,
    d_send,
    d_recv,
    i_sem,
):
    xh = lax.axis_index("xh")
    y = lax.axis_index("y")
    c = lax.axis_index("c")
    xl = lax.axis_index("xl")
    z = lax.axis_index("z")
    me = xh * 8 + y
    seq = me * 2 + c
    doc = xl * 8 + z
    sig = 1 - 2 * lax.rem(z, 2)
    z_up = lax.rem(z + sig + 8, 8)
    z_dn = lax.rem(z - sig + 8, 8)
    z_pair = z + sig

    fetches = [
        pltpu.make_async_copy(src, dst, i_sem.at[n])
        for n, (src, dst) in enumerate(
            (
                (base_in.at[lax.axis_index("xh") * 16 + lax.axis_index("y") * 2 + lax.axis_index("c")], base_ref),
                (step_in, step_ref),
                (k_in, k_ref),
                (q_in, q_ref),
                (v_in, v_ref),
                (hid_in, hid_ref),
                (ow_in, ow_ref),
                (gain_in, gain_ref),
                (lengths_in, lengths_ref),
                (rank_in, rank_ref),
                (tgt_ref, tgts.at[0]),
            )
        )
    ]
    for fetch in fetches:
        fetch.start()
    barrier = pltpu.get_barrier_semaphore()

    def peer_seq(k):
        n = lax.rem(seq + k, SEQ)
        return {"xh": lax.div(n, 16), "y": lax.rem(lax.div(n, 2), 8), "c": lax.rem(n, 2)}

    def peer_doc(k):
        n = lax.rem(doc + k, DOCS)
        return {"xl": lax.div(n, 8), "z": lax.rem(n, 8)}

    for k in range(1, SEQ):
        pl.semaphore_signal(barrier, inc=1, device_id=peer_seq(k), device_id_type=MESH)
    for k in range(1, DOCS):
        pl.semaphore_signal(barrier, inc=1, device_id=peer_doc(k), device_id_type=MESH)

    mine = pltpu.make_async_copy(un_ref, wide.at[:, pl.ds(0, SHARE)], w_sem.at[4])
    mine.start()

    lane = lanes((ROWS, ROWS))
    low = lane < HEAD_DIM
    first = lax.rem(lane, HEAD_DIM) < ROT // 2
    low_half = low[:HEAD_DIM]

    for fetch in fetches[:5]:
        fetch.wait()

    base_cos = base_ref[0:1]
    base_sin = base_ref[1:2]
    cosine = base_cos * step_ref[0] - base_sin * step_ref[1]
    sine = base_sin * step_ref[0] + base_cos * step_ref[1]
    sine = jnp.where(first, -sine, sine)

    def turn(block):
        partner = jnp.where(first, pltpu.roll(block, ROWS - 8, 1), pltpu.roll(block, 8, 1))
        return block * cosine + partner * sine

    for pair in range(HEADS // 2):
        at = slice(pair * ROWS, (pair + 1) * ROWS)
        tk = turn(k_ref[:, at].astype(F32))
        tq = turn(q_ref[:, at].astype(F32))
        tv = v_ref[:, at].astype(F32)
        rk = pltpu.roll(tk, HEAD_DIM, 1)
        rq = pltpu.roll(tq, HEAD_DIM, 1)
        rv = pltpu.roll(tv, HEAD_DIM, 1)
        packed[2 * pair, 0:ROWS] = jnp.where(low, tk, rv).astype(BF16)
        packed[2 * pair + 1, 0:ROWS] = jnp.where(low, rk, tv).astype(BF16)
        packed[2 * pair, ROWS : ROWS + HEAD_DIM] = jnp.where(
            low_half, tq[:HEAD_DIM], rq[HEAD_DIM:]
        ).astype(BF16)
        packed[2 * pair + 1, ROWS : ROWS + HEAD_DIM] = jnp.where(
            low_half, rq[:HEAD_DIM], tq[HEAD_DIM:]
        ).astype(BF16)

    pl.semaphore_wait(barrier, SEQ - 1 + DOCS - 1)

    half_rows = pl.ds(pl.multiple_of(c * (D // 2), D // 2), D // 2)
    swap = rcopy(
        un_ref.at[half_rows],
        wide.at[half_rows, pl.ds(SHARE, SHARE)],
        w_sem.at[0],
        w_sem.at[1],
        z=z_pair,
    )
    swap.start()

    is_head = jnp.logical_and(y != 3, y != 7)
    my_slot = y - jnp.where(y > 3, 1, 0)
    my_head = jnp.where(is_head, xh * 6 + my_slot, -1)

    start = lax.rem(my_head, 4)
    my_group = lax.div(me, 4)

    def head_copy(h):
        yi = lax.rem(h, 6)
        return rcopy(
            packed.at[h],
            got.at[c, me],
            a_send.at[0],
            a_recv.at[my_group],
            xh=h // 6,
            y=yi + jnp.where(yi > 2, 1, 0),
        )

    def send_head(n, carry):
        h = 4 * lax.rem(n + me, 3) + lax.rem(my_group + 4 - n // 3, 4)

        @pl.when(h != my_head)
        def _():
            head_copy(h).start()

        @pl.when(h == my_head)
        def _():
            got[c, me] = packed[h]

        return carry

    lax.fori_loop(0, HEADS, send_head, 0)

    def target_copy(n):
        side = lax.rem(n, 2)
        step = n // 2
        move = jnp.where(
            step == 0, 0, jnp.where(step == 1, -sig, jnp.where(step == 2, 2 * sig, -3 * sig))
        )
        return rcopy(
            tgt_ref,
            tgts.at[n],
            t_send.at[0],
            t_recv.at[0],
            xl=lax.rem(xl + side, 2),
            z=lax.rem(z + move + 8, 8),
        )

    def send_target(n, carry):
        target_copy(n).start()
        return carry

    lax.fori_loop(1, 8, send_target, 0)

    def arrival(g):
        def wait(count):
            part = got.at[c, pl.ds(4 * g, count)]
            rcopy(part, part, a_send.at[0], a_recv.at[g], xh=xh, y=y).wait_recv()

        @pl.when(g != my_group)
        def _():
            wait(4)

        @pl.when(g == my_group)
        def _():
            wait(3)

    def forward(g):
        part = got.at[c, pl.ds(4 * g, 4), pl.ds(0, ROWS)]
        return rcopy(part, part, f_send.at[g], f_recv.at[g], c=1 - c)

    def forwarded(g):
        part = got.at[1 - c, pl.ds(4 * g, 4), pl.ds(0, ROWS)]
        return rcopy(part, part, f_send.at[g], f_recv.at[g], c=1 - c)

    scale = LOG2E / math.sqrt(HEAD_DIM)

    def result_copy(i):
        return rcopy(
            outs.at[i],
            att.at[my_head],
            r_send.at[0],
            r_recv.at[0],
            xh=i // 8,
            y=lax.rem(i, 8),
        )

    def pair_of(gq, gk, masked):
        block = got[:, pl.ds(4 * gk, 4), 0:ROWS, :].reshape(CHUNK, ROWS)
        s = lax.dot_general(
            qt[gq], block, (((1,), (1,)), ((), ())), preferred_element_type=F32
        )
        if masked:
            shape = (SPAN, CHUNK)
            row = rows_of(shape)
            col = lanes(shape)
            later = col >= SPAN
            key = jnp.where(later, col - SPAN, col)
            key = key + (key // ROWS) * ROWS + jnp.where(later, ROWS, 0)
            s = jnp.where(key <= row + (row // ROWS) * ROWS + c * ROWS, s, NEGATIVE)
        s_scr[...] = s
        top = s[:, 0:ROWS]
        for g in range(1, CHUNK // ROWS):
            top = jnp.maximum(top, s[:, g * ROWS : (g + 1) * ROWS])
        old = mx_ref[gq]
        top = jnp.maximum(old, jnp.max(top, axis=1, keepdims=True) * scale)
        mx_ref[gq] = top
        factor = jnp.exp2(old - top)
        total = sum_ref[gq] * factor
        parts = []
        for g in range(CHUNK // ROWS):
            p = jnp.exp2(s_scr[:, g * ROWS : (g + 1) * ROWS] * scale - top)
            total = total + p
            parts.append(p.astype(BF16))
        sum_ref[gq] = total
        p = jnp.concatenate(parts, axis=1)
        pv_ref[gq] = pv_ref[gq] * factor + jnp.dot(p, block, preferred_element_type=F32)

    def finish(gq):
        out = pv_ref[gq] / jnp.sum(sum_ref[gq], axis=1, keepdims=True)
        for u in range(4):
            i = 4 * gq + u
            top_part = out[u * ROWS : u * ROWS + HEAD_DIM]
            bottom = out[u * ROWS + HEAD_DIM : (u + 1) * ROWS]
            whole = jnp.where(low_half, pltpu.roll(top_part, HEAD_DIM, 1), bottom).astype(BF16)
            outs[i] = whole

            @pl.when(i != me)
            def _():
                result_copy(i).start()

            @pl.when(i == me)
            def _():
                att[my_head] = whole

    def phase(p, carry):
        g = lax.rem(start + p, 4)
        arrival(g)
        forward(g).start()
        for u in range(4):
            qp = got[c, 4 * g + u, ROWS : ROWS + HEAD_DIM].astype(F32)
            qt[g, u * ROWS : u * ROWS + HEAD_DIM] = jnp.where(low_half, qp, 0.0).astype(BF16)
            qt[g, u * ROWS + HEAD_DIM : (u + 1) * ROWS] = jnp.where(
                low_half, pltpu.roll(qp, HEAD_DIM, 1), 0.0
            ).astype(BF16)
        mx_ref[g] = jnp.full((SPAN, ROWS), NEGATIVE, F32)
        sum_ref[g] = jnp.zeros((SPAN, ROWS), F32)
        pv_ref[g] = jnp.zeros((SPAN, ROWS), F32)
        forwarded(g).wait_recv()

        def visit(m, inner):
            other = lax.rem(start + m, 4)
            gq = jnp.maximum(g, other)
            gk = jnp.minimum(g, other)

            @pl.when(m < p)
            def _():
                pair_of(gq, gk, False)

            @pl.when(m == p)
            def _():
                pair_of(g, g, True)

            ready = jnp.where(gq < start, gq + 4 - start, jnp.where(start == 0, gq, 3))

            @pl.when(jnp.logical_and(p == ready, jnp.logical_or(m == p, gq != g)))
            def _():
                finish(gq)

            return inner

        lax.fori_loop(0, p + 1, visit, 0)
        return carry

    @pl.when(is_head)
    def _():
        lax.fori_loop(0, 4, phase, 0)

    swap.wait_recv()
    share = wide.at[half_rows, pl.ds(SHARE, SHARE)]
    pass_on = rcopy(share, share, w_sem.at[2], w_sem.at[3], c=1 - c)
    pass_on.start()

    @pl.when(is_head)
    def _():
        part = att.at[pl.ds(0, HEADS - 1)]
        rcopy(part, part, r_send.at[0], r_recv.at[0], xh=xh, y=y).wait_recv()

    @pl.when(jnp.logical_not(is_head))
    def _():
        rcopy(att, att, r_send.at[0], r_recv.at[0], xh=xh, y=y).wait_recv()

    for fetch in fetches[5:]:
        fetch.wait()
    for pair in range(HEADS // 2):
        at = slice(pair * ROWS, (pair + 1) * ROWS)
        even = att[2 * pair].astype(F32)
        odd = att[2 * pair + 1].astype(F32)
        attended[0:HEAD_DIM, at] = jnp.where(
            low_half, even, pltpu.roll(odd, HEAD_DIM, 1)
        ).astype(BF16)
        attended[HEAD_DIM:ROWS, at] = jnp.where(
            low_half, pltpu.roll(even, HEAD_DIM, 1), odd
        ).astype(BF16)
    residual = hid_ref[...].astype(F32) + jnp.dot(
        attended[...], ow_ref[...], preferred_element_type=F32
    )
    center = residual - jnp.sum(residual, axis=1, keepdims=True) * (1.0 / D)
    spread = jnp.sum(center * center, axis=1, keepdims=True) * (1.0 / D)
    rows_buf[0] = (center * lax.rsqrt(spread + NORM_EPSILON) * gain_ref[...].reshape(1, D)).astype(BF16)

    def row_copy(n):
        if n < 4:
            return rcopy(
                rows_buf.at[2 * n],
                rows_buf.at[2 * n + 1],
                c_send.at[n],
                c_recv.at[2 * n + 1],
                xl=1 - xl,
            )
        if n == 4:
            return rcopy(rows_buf.at[0], rows_buf.at[2], c_send.at[4], c_recv.at[2], z=z_dn)
        if n == 5:
            return rcopy(rows_buf.at[0], relay.at[0], c_send.at[5], c_recv.at[8], z=z_up)
        if n == 6:
            return rcopy(rows_buf.at[2], relay.at[1], c_send.at[6], c_recv.at[9], z=z_up)
        if n == 7:
            return rcopy(relay.at[0], rows_buf.at[4], c_send.at[7], c_recv.at[4], z=z_dn)
        return rcopy(relay.at[1], rows_buf.at[6], c_send.at[8], c_recv.at[6], z=z_dn)

    def row_wait(slot):
        ref = relay.at[slot - 8] if slot >= 8 else rows_buf.at[slot]
        rcopy(rows_buf.at[0], ref, c_send.at[0], c_recv.at[slot], z=z_dn).wait_recv()

    row_copy(4).start()
    row_copy(5).start()
    row_copy(0).start()
    mine.wait()
    pass_on.wait_recv()

    part = tgts.at[pl.ds(1, 7)]
    rcopy(part, part, t_send.at[0], t_recv.at[0], z=z_dn).wait_recv()
    diagonal = lane == rows_of((ROWS, ROWS))
    other = xl * 8 + z_pair

    def stat_copy(slot):
        side = lax.rem(slot, 2)
        back = lax.rem(z - sig * (slot // 2) + 8, 8)
        return rcopy(
            stat_out.at[slot],
            stats.at[xl * 4 + z // 2],
            s_send.at[0],
            s_recv.at[0],
            xl=lax.rem(xl + side, 2),
            z=back,
        )

    def as_row(column):
        return jnp.sum(jnp.where(diagonal, column, 0.0), axis=0, keepdims=True)

    def score_rows(n, carry):
        @pl.when(n == 0)
        def _():
            row_wait(1)
            row_wait(2)
            row_copy(6).start()
            row_copy(1).start()
            row_wait(8)
            row_copy(7).start()

        @pl.when(n == 1)
        def _():
            row_wait(9)
            row_copy(8).start()
            row_wait(4)
            row_copy(2).start()
            row_wait(3)

        @pl.when(n == 2)
        def _():
            row_wait(6)
            row_copy(3).start()
            row_wait(5)

        @pl.when(n == 3)
        def _():
            row_wait(7)

        block = rows_buf[pl.ds(2 * n, 2)].reshape(2 * ROWS, D)
        top = jnp.full((2 * ROWS, ROWS), NEGATIVE, F32)
        for k in range(TILES):
            s = jnp.dot(
                block, wide[:, k * TILE : (k + 1) * TILE], preferred_element_type=F32
            )
            logit[k] = s
            top = jnp.maximum(top, jnp.maximum(s[:, :ROWS], s[:, ROWS:]))

        def placed(slot):
            wanted = jnp.broadcast_to(tgts[slot], (ROWS, ROWS))
            wanted = jnp.sum(
                jnp.where(diagonal, wanted.astype(F32), 0.0), axis=1, keepdims=True
            ).astype(jnp.int32)
            here = wanted - doc * SHARE
            there = wanted - other * SHARE
            spot = jnp.where(
                jnp.logical_and(here >= 0, here < SHARE),
                here,
                jnp.where(jnp.logical_and(there >= 0, there < SHARE), there + SHARE, -1),
            )
            return jnp.broadcast_to(spot, (ROWS, ROWS)) - lane

        place = jnp.concatenate([placed(2 * n), placed(2 * n + 1)], axis=0)
        top = jnp.max(top, axis=1, keepdims=True)
        top2 = jnp.broadcast_to(top * LOG2E, (2 * ROWS, ROWS))
        sum_ref[0, 0 : 2 * ROWS] = jnp.zeros((2 * ROWS, ROWS), F32)
        pv_ref[0, 0 : 2 * ROWS] = jnp.zeros((2 * ROWS, ROWS), F32)

        def add_up(k, inner):
            total = sum_ref[0, 0 : 2 * ROWS]
            pick = pv_ref[0, 0 : 2 * ROWS]
            for g in range(TILE // ROWS):
                s = logit[k, :, g * ROWS : (g + 1) * ROWS]
                total = total + jnp.exp2(s * LOG2E - top2)
                pick = pick + jnp.where(place == k * TILE + g * ROWS, s, 0.0)
            sum_ref[0, 0 : 2 * ROWS] = total
            pv_ref[0, 0 : 2 * ROWS] = pick
            return inner

        lax.fori_loop(0, TILES, add_up, 0)
        lse = top + jnp.log(jnp.sum(sum_ref[0, 0 : 2 * ROWS], axis=1, keepdims=True))
        pick = jnp.sum(pv_ref[0, 0 : 2 * ROWS], axis=1, keepdims=True)
        row8 = rows_of((8, ROWS))
        tiles = [
            jnp.where(row8 == 0, as_row(lse[at : at + ROWS]), as_row(pick[at : at + ROWS]))
            for at in (0, ROWS)
        ]
        stat_out[2 * n + 1] = tiles[1]
        stat_copy(2 * n + 1).start()

        @pl.when(n != 0)
        def _():
            stat_out[2 * n] = tiles[0]
            stat_copy(2 * n).start()

        @pl.when(n == 0)
        def _():
            stats[xl * 4 + z // 2] = tiles[0]

        return carry

    lax.fori_loop(0, 4, score_rows, 0)

    part = stats.at[pl.ds(0, 7)]
    rcopy(part, part, s_send.at[0], s_recv.at[0], z=z_dn).wait_recv()
    parts = [stats[n] for n in range(8)]
    top = parts[0][0:1]
    for part in parts[1:]:
        top = jnp.maximum(top, part[0:1])
    total = jnp.zeros((1, ROWS), F32)
    pick = jnp.zeros((1, ROWS), F32)
    for part in parts:
        total = total + jnp.exp(part[0:1] - top)
        pick = pick + part[1:2]
    place = seq * ROWS + lanes((1, ROWS))
    nll = jnp.where(place < lengths_ref[doc], top + jnp.log(total) - pick, 0.0)
    seqs[seq] = jnp.broadcast_to(jnp.sum(nll, axis=1, keepdims=True), (1, ROWS))

    for k in range(1, SEQ):
        rcopy(seqs.at[seq], seqs.at[seq], q_send.at[0], q_recv.at[0], **peer_seq(k)).start()

    @pl.when(is_head)
    def _():
        part = packed.at[pl.ds(0, HEADS - 1)]
        rcopy(part, part, a_send.at[0], a_recv.at[0], xh=xh, y=y).wait_send()
        part = outs.at[pl.ds(0, 15)]
        rcopy(part, part, r_send.at[0], r_recv.at[0], xh=xh, y=y).wait_send()
        for g in range(4):
            forward(g).wait_send()

    @pl.when(jnp.logical_not(is_head))
    def _():
        rcopy(packed, packed, a_send.at[0], a_recv.at[0], xh=xh, y=y).wait_send()

    swap.wait_send()
    pass_on.wait_send()
    for n in range(9):
        row_copy(n).wait_send()
    part = tgts.at[pl.ds(1, 7)]
    rcopy(part, part, t_send.at[0], t_recv.at[0], z=z_dn).wait_send()
    part = stat_out.at[pl.ds(1, 7)]
    rcopy(part, part, s_send.at[0], s_recv.at[0], z=z_dn).wait_send()
    others = seqs.at[pl.ds(0, SEQ - 1)]
    rcopy(others, others, q_send.at[0], q_recv.at[0], z=z_dn).wait_recv()
    docs[doc] = jnp.sum(seqs[...], axis=0)

    for k in range(1, DOCS):
        rcopy(docs.at[doc], docs.at[doc], d_send.at[0], d_recv.at[0], **peer_doc(k)).start()
    rcopy(others, others, q_send.at[0], q_recv.at[0], z=z_dn).wait_send()
    part = docs.at[pl.ds(0, DOCS - 1)]
    rcopy(part, part, d_send.at[0], d_recv.at[0], z=z_dn).wait_recv()

    shape = (DOCS, ROWS)
    row = rows_of(shape)
    col = lanes(shape)
    column = docs[...].reshape(DOCS, ROWS)
    for d in range(DOCS):
        column = jnp.where(row == d, column / lengths_ref[d].astype(F32), column)
    valid = lanes((1, ROWS)) < DOCS
    line = jnp.sum(jnp.where(row == col, column, 0.0), axis=0, keepdims=True)
    mean = jnp.sum(line, axis=1, keepdims=True) * (1.0 / DOCS)
    off = jnp.where(valid, line - mean, 0.0)
    spread = jnp.sqrt(jnp.sum(off * off, axis=1, keepdims=True) * (1.0 / DOCS) + SPREAD_EPSILON)
    ahead = jnp.logical_or(
        column < line, jnp.logical_and(column == line, row < col)
    )
    rank = jnp.sum(jnp.where(ahead, 1.0, 0.0), axis=0, keepdims=True)
    scaled = rank_ref[0] * (DOCS - 1)
    low_index = lax.div(scaled, 99)
    high_index = jnp.minimum(low_index + 1, DOCS - 1)
    fraction = (scaled - 99 * low_index).astype(F32) / 99.0
    hit_low = jnp.logical_and(valid, rank == low_index.astype(F32))
    hit_high = jnp.logical_and(valid, rank == high_index.astype(F32))
    low_value = jnp.sum(jnp.where(hit_low, line, 0.0), axis=1, keepdims=True)
    high_value = jnp.sum(jnp.where(hit_high, line, 0.0), axis=1, keepdims=True)
    level = (1.0 - fraction) * low_value + fraction * high_value
    accepted = jax.nn.sigmoid((level - line) / spread)
    row = rows_of((8, ROWS))
    final_ref[...] = jnp.where(row == 0, nll, jnp.where(row == 1, line, accepted))
    rcopy(part, part, d_send.at[0], d_recv.at[0], z=z_dn).wait_send()


def split_kernel(final_ref, nll_ref, ppl_ref, acc_ref):
    nll_ref[...] = final_ref[0:1]
    ppl_ref[...] = final_ref[1:2, :DOCS]
    acc_ref[...] = final_ref[2:3, :DOCS]


def turn_tables():
    spot = np.arange(ROWS) % HEAD_DIM
    freq = ROTARY_BASE ** (-2.0 * (spot % (ROT // 2)) / ROT)
    freq = np.where(spot < ROT, freq, 0.0)
    base = np.arange(SEQ)[:, None] * float(ROWS) * freq[None, :]
    step = np.arange(ROWS)[:, None] * freq[None, :]
    base = np.stack([np.cos(base), np.sin(base)], axis=1).astype(np.float32)
    step = np.stack([np.cos(step), np.sin(step)], axis=0).astype(np.float32)
    return base, step


def shards(
    hidden,
    queries,
    key_states,
    values,
    targets,
    lengths,
    keep_rank,
    out_weight,
    final_gain,
    unembed,
):
    base, step = turn_tables()
    vmem = pl.BlockSpec(memory_space=pltpu.VMEM)
    dma = pltpu.SemaphoreType.DMA
    final = pl.pallas_call(
        kernel,
        name="scoring",
        out_shape=jax.ShapeDtypeStruct((8, ROWS), F32),
        in_specs=[pl.BlockSpec(memory_space=pltpu.HBM)] * 12,
        out_specs=vmem,
        scratch_shapes=[
            pltpu.VMEM((2, ROWS), F32),
            pltpu.VMEM((2, ROWS, ROWS), F32),
            pltpu.SMEM((DOCS,), jnp.int32),
            pltpu.SMEM((1,), jnp.int32),
            pltpu.VMEM((ROWS, D), BF16),
            pltpu.VMEM((ROWS, D), BF16),
            pltpu.VMEM((ROWS, D), BF16),
            pltpu.VMEM((ROWS, D), BF16),
            pltpu.VMEM((D,), F32),
            pltpu.VMEM((D, D), BF16),
            pltpu.VMEM((HEADS, ROWS + HEAD_DIM, ROWS), BF16),
            pltpu.VMEM((2, 16, ROWS + HEAD_DIM, ROWS), BF16),
            pltpu.VMEM((16, HEAD_DIM, ROWS), BF16),
            pltpu.VMEM((HEADS, HEAD_DIM, ROWS), BF16),
            pltpu.VMEM((ROWS, D), BF16),
            pltpu.VMEM((4, SPAN, ROWS), BF16),
            pltpu.VMEM((SPAN, CHUNK), F32),
            pltpu.VMEM((4, SPAN, ROWS), F32),
            pltpu.VMEM((4, SPAN, ROWS), F32),
            pltpu.VMEM((4, SPAN, ROWS), F32),
            pltpu.VMEM((D, WIDE), BF16),
            pltpu.VMEM((8, ROWS, D), BF16),
            pltpu.VMEM((2, ROWS, D), BF16),
            pltpu.VMEM((TILES, 2 * ROWS, TILE), F32),
            pltpu.VMEM((8, 1, ROWS), jnp.int32),
            pltpu.VMEM((8, 8, ROWS), F32),
            pltpu.VMEM((8, 8, ROWS), F32),
            pltpu.VMEM((SEQ, 1, ROWS), F32),
            pltpu.VMEM((DOCS, 1, ROWS), F32),
            dma((1,)),
            dma((4,)),
            dma((4,)),
            dma((4,)),
            dma((1,)),
            dma((1,)),
            dma((5,)),
            dma((9,)),
            dma((10,)),
            dma((1,)),
            dma((1,)),
            dma((1,)),
            dma((1,)),
            dma((1,)),
            dma((1,)),
            dma((1,)),
            dma((1,)),
            dma((11,)),
        ],
        compiler_params=pltpu.CompilerParams(
            collective_id=0, has_side_effects=True, vmem_limit_bytes=67043328
        ),
    )(
        jnp.asarray(base),
        jnp.asarray(step),
        lengths,
        keep_rank,
        queries[0],
        key_states[0],
        values[0],
        hidden[0],
        targets,
        final_gain,
        out_weight,
        unembed,
    )
    nll, ppl, acceptance = pl.pallas_call(
        split_kernel,
        name="split",
        out_shape=(
            jax.ShapeDtypeStruct((1, ROWS), F32),
            jax.ShapeDtypeStruct((1, DOCS), F32),
            jax.ShapeDtypeStruct((1, DOCS), F32),
        ),
        in_specs=[vmem],
        out_specs=(vmem, vmem, vmem),
    )(final)
    return (nll, ppl.reshape(DOCS), acceptance.reshape(DOCS))


def solution(mesh):
    split = Mesh(mesh.devices.reshape(2, 8, 2, 2, 8), ("xh", "y", "c", "xl", "z"))
    rows = ("xh", "y", "c")
    parts = ("xl", "z")
    placed = (
        P(parts, rows, None),
        P(parts, rows, None),
        P(parts, rows, None),
        P(parts, rows, None),
        P(parts, rows),
        P(),
        P(),
        P(),
        P(),
        P(None, parts),
    )
    return jax.shard_map(
        shards, mesh=split, in_specs=placed, out_specs=(P(parts, rows), P(), P()), check_vma=False
    )
```

time: 125 us -> 95.2 us (0.76)
  Pallas kernels: 112 us -> 93.8 us
  local copies, waits for them, and re-layouts: 9.57 us -> 0 us
    pallas_call x1 -> x2, Pallas kernels: 112 us -> 93.8 us  [the longest x1 92.6 us: shards(): pl.pallas_call(kernel, name='scoring', out_shape=jax.ShapeDtypeStruct((8,...]
    unnamed x15 -> x0, local copies, waits for them, and re-layouts: 7.86 us -> none
where the time goes in v2:
time: 95.2 us; the launch traced here: 95.1 us
  Pallas kernels  93.8 us (99%)
  between operations  1.29 us (1%)
    pallas_call x1, Pallas kernels, shards(): pl.pallas_call(kernel, name='scoring', out_shape=jax.ShapeDtypeStruct((8,...  92.6 us

profile of v2, /device:TPU:1, one launch (start us, length us, event | category | flops | bytes accessed | tf_op | source)
XLA Modules:
  0.0 95.1 jit_solution(8610056293351916326)
XLA Ops:
  1.3 92.6 %scoring.1.final_ref = f32[8,128]{1,0:T(8,128)} custom-call(f32[32,2,128]{2,1,0:T(2,128)} %constant.4.clone.base_in, f32[2,128,128]{2,1,0:T(8,128)} %constant.5.clone.step_in, s32[16]{0:T(128)} %lengths_in.1, s32[1]{0:T(128)S(6)} %copy.15.rank_in, bf16[128,768]{1,0:T(8,128)(2,1)} %bitcast.6, bf16[128,768]{1,0:T(8,128)(2,1)} %bitcast.7, ...), custom_call_target="tpu_custom_call" | custom-call | tf_op jit(solution)/shard_map/scoring/pallas_call | solution.py:677
  93.9 1.2 %split.1 = (f32[1,128]{1,0:T(1,128)}, f32[1,16]{1,0:T(1,128)}, f32[1,16]{1,0:T(1,128)}) custom-call(f32[8,128]{1,0:T(8,128)} %scoring.1.final_ref), custom_call_target="tpu_custom_call" | custom-call | tf_op jit(solution)/shard_map/split/pallas_call | solution.py:749

commit v3 on v2

--- a/solution.py
+++ b/solution.py
@@ -20,7 +20,7 @@
 TILES = WIDE // TILE
 DOCS = 16
 SEQ = 32
-CHUNK = 1024
+HALF = 256
 SPAN = 512
 NEGATIVE = -1e30
 ROTARY_BASE = 10000.0
@@ -79,12 +79,14 @@
     got,
     outs,
     att,
-    attended,
     qt,
+    vt,
     s_scr,
     mx_ref,
     sum_ref,
     pv_ref,
+    v_sum,
+    v_pick,
     wide,
     rows_buf,
     relay,
@@ -93,7 +95,6 @@
     stat_out,
     stats,
     seqs,
-    docs,
     a_send,
     a_recv,
     f_send,
@@ -109,9 +110,9 @@
     s_recv,
     q_send,
     q_recv,
-    d_send,
-    d_recv,
     i_sem,
+    tie_buf,
+    tie_sem,
 ):
     xh = lax.axis_index("xh")
     y = lax.axis_index("y")
@@ -126,11 +127,26 @@
     z_dn = lax.rem(z - sig + 8, 8)
     z_pair = z + sig
 
+    barrier = pltpu.get_barrier_semaphore()
+
+    def peer_seq(k):
+        n = lax.rem(seq + k, SEQ)
+        return {"xh": lax.div(n, 16), "y": lax.rem(lax.div(n, 2), 8), "c": lax.rem(n, 2)}
+
+    def peer_doc(k):
+        n = lax.rem(doc + k, DOCS)
+        return {"xl": lax.div(n, 8), "z": lax.rem(n, 8)}
+
+    for k in range(1, SEQ):
+        pl.semaphore_signal(barrier, inc=1, device_id=peer_seq(k), device_id_type=MESH)
+    for k in range(1, DOCS):
+        pl.semaphore_signal(barrier, inc=1, device_id=peer_doc(k), device_id_type=MESH)
+
     fetches = [
         pltpu.make_async_copy(src, dst, i_sem.at[n])
         for n, (src, dst) in enumerate(
             (
-                (base_in.at[lax.axis_index("xh") * 16 + lax.axis_index("y") * 2 + lax.axis_index("c")], base_ref),
+                (base_in.at[seq], base_ref),
                 (step_in, step_ref),
                 (k_in, k_ref),
                 (q_in, q_ref),
@@ -146,21 +162,6 @@
     ]
     for fetch in fetches:
         fetch.start()
-    barrier = pltpu.get_barrier_semaphore()
-
-    def peer_seq(k):
-        n = lax.rem(seq + k, SEQ)
-        return {"xh": lax.div(n, 16), "y": lax.rem(lax.div(n, 2), 8), "c": lax.rem(n, 2)}
-
-    def peer_doc(k):
-        n = lax.rem(doc + k, DOCS)
-        return {"xl": lax.div(n, 8), "z": lax.rem(n, 8)}
-
-    for k in range(1, SEQ):
-        pl.semaphore_signal(barrier, inc=1, device_id=peer_seq(k), device_id_type=MESH)
-    for k in range(1, DOCS):
-        pl.semaphore_signal(barrier, inc=1, device_id=peer_doc(k), device_id_type=MESH)
-
     mine = pltpu.make_async_copy(un_ref, wide.at[:, pl.ds(0, SHARE)], w_sem.at[4])
     mine.start()
 
@@ -229,10 +230,36 @@
             y=yi + jnp.where(yi > 2, 1, 0),
         )
 
+    tie_y = lax.rem(y + 4, 8)
+    has_tie = jnp.logical_and(tie_y != 3, tie_y != 7)
+    tie_head = jnp.where(has_tie, xh * 6 + tie_y - jnp.where(tie_y > 3, 1, 0), -1)
+    tie_from = xh * 8 + lax.rem(y + 3, 8)
+    relays = jnp.logical_and(y != 4, y != 0)
+    tie_send = rcopy(
+        packed.at[jnp.maximum(tie_head, 0)],
+        tie_buf,
+        a_send.at[0],
+        tie_sem.at[0],
+        xh=xh,
+        y=lax.rem(y + 5, 8),
+    )
+    tie_pass = rcopy(
+        tie_buf,
+        got.at[c, tie_from],
+        tie_sem.at[1],
+        a_recv.at[lax.div(tie_from, 4)],
+        xh=xh,
+        y=lax.rem(y + 7, 8),
+    )
+
+    @pl.when(has_tie)
+    def _():
+        tie_send.start()
+
     def send_head(n, carry):
         h = 4 * lax.rem(n + me, 3) + lax.rem(my_group + 4 - n // 3, 4)
 
-        @pl.when(h != my_head)
+        @pl.when(jnp.logical_and(h != my_head, h != tie_head))
         def _():
             head_copy(h).start()
 
@@ -265,6 +292,11 @@
 
     lax.fori_loop(1, 8, send_target, 0)
 
+    @pl.when(relays)
+    def _():
+        tie_send.wait_recv()
+        tie_pass.start()
+
     def arrival(g):
         def wait(count):
             part = got.at[c, pl.ds(4 * g, count)]
@@ -298,68 +330,81 @@
             y=lax.rem(i, 8),
         )
 
-    def pair_of(gq, gk, masked):
-        block = got[:, pl.ds(4 * gk, 4), 0:ROWS, :].reshape(CHUNK, ROWS)
-        s = lax.dot_general(
-            qt[gq], block, (((1,), (1,)), ((), ())), preferred_element_type=F32
-        )
-        if masked:
-            shape = (SPAN, CHUNK)
-            row = rows_of(shape)
-            col = lanes(shape)
-            later = col >= SPAN
-            key = jnp.where(later, col - SPAN, col)
-            key = key + (key // ROWS) * ROWS + jnp.where(later, ROWS, 0)
-            s = jnp.where(key <= row + (row // ROWS) * ROWS + c * ROWS, s, NEGATIVE)
-        s_scr[...] = s
-        top = s[:, 0:ROWS]
-        for g in range(1, CHUNK // ROWS):
-            top = jnp.maximum(top, s[:, g * ROWS : (g + 1) * ROWS])
-        old = mx_ref[gq]
-        top = jnp.maximum(old, jnp.max(top, axis=1, keepdims=True) * scale)
-        mx_ref[gq] = top
-        factor = jnp.exp2(old - top)
-        total = sum_ref[gq] * factor
-        parts = []
-        for g in range(CHUNK // ROWS):
-            p = jnp.exp2(s_scr[:, g * ROWS : (g + 1) * ROWS] * scale - top)
-            total = total + p
-            parts.append(p.astype(BF16))
-        sum_ref[gq] = total
-        p = jnp.concatenate(parts, axis=1)
-        pv_ref[gq] = pv_ref[gq] * factor + jnp.dot(p, block, preferred_element_type=F32)
+    def pair_of(gq, gk, diagonal):
+        blocks = [(uh, par) for uh in range(2) for par in range(2)]
+        tops = []
+        for hq in range(2):
+            queries = qt[gq, hq * HALF : (hq + 1) * HALF]
+            top = jnp.full((8, HALF), NEGATIVE, F32)
+            for b, (uh, par) in enumerate(blocks):
+                if diagonal and uh > hq:
+                    continue
+                keys = got[par, pl.ds(4 * gk + 2 * uh, 2), 0:ROWS, :].reshape(HALF, ROWS)
+                s = lax.dot_general(
+                    keys, queries, (((1,), (1,)), ((), ())), preferred_element_type=F32
+                )
+                if diagonal and uh == hq:
+                    row = rows_of((HALF, HALF))
+                    col = lanes((HALF, HALF))
+                    key = row + jnp.where(row >= ROWS, ROWS, 0) + par * ROWS
+                    query = col + jnp.where(col >= ROWS, ROWS, 0) + c * ROWS
+                    s = jnp.where(key <= query, s, NEGATIVE)
+                s_scr[hq, b] = s
+                top = jnp.maximum(top, jnp.max(s.reshape(HALF // 8, 8, HALF), axis=0))
+            tops.append(top)
+        for hq in range(2):
+            old = mx_ref[gq, hq]
+            new = jnp.maximum(old, jnp.max(tops[hq], axis=0, keepdims=True) * scale)
+            mx_ref[gq, hq] = new
+            factor = jnp.exp2(old - new)
+            total = sum_ref[gq, hq] * factor
+            parts = []
+            count = 2 if diagonal and hq == 0 else 4
+            for b in range(count):
+                p = jnp.exp2(s_scr[hq, b] * scale - new)
+                total = total + jnp.sum(p.reshape(HALF // 8, 8, HALF), axis=0)
+                parts.append(p.astype(BF16))
+            sum_ref[gq, hq] = total
+            pv_ref[gq, hq] = pv_ref[gq, hq] * factor + jnp.dot(
+                vt[gk, :, 0 : count * HALF],
+                jnp.concatenate(parts, axis=0),
+                preferred_element_type=F32,
+            )
 
     def finish(gq):
-        out = pv_ref[gq] / jnp.sum(sum_ref[gq], axis=1, keepdims=True)
-        for u in range(4):
-            i = 4 * gq + u
-            top_part = out[u * ROWS : u * ROWS + HEAD_DIM]
-            bottom = out[u * ROWS + HEAD_DIM : (u + 1) * ROWS]
-            whole = jnp.where(low_half, pltpu.roll(top_part, HEAD_DIM, 1), bottom).astype(BF16)
-            outs[i] = whole
-
-            @pl.when(i != me)
-            def _():
-                result_copy(i).start()
-
-            @pl.when(i == me)
-            def _():
-                att[my_head] = whole
+        for hq in range(2):
+            out = pv_ref[gq, hq] / jnp.sum(sum_ref[gq, hq], axis=0, keepdims=True)
+            for u in range(2):
+                i = 4 * gq + 2 * hq + u
+                whole = out[:, u * ROWS : (u + 1) * ROWS].astype(BF16)
+                outs[i] = whole
+
+                @pl.when(i != me)
+                def _():
+                    result_copy(i).start()
+
+                @pl.when(i == me)
+                def _():
+                    att[my_head] = whole
 
     def phase(p, carry):
         g = lax.rem(start + p, 4)
-        arrival(g)
-        forward(g).start()
         for u in range(4):
             qp = got[c, 4 * g + u, ROWS : ROWS + HEAD_DIM].astype(F32)
             qt[g, u * ROWS : u * ROWS + HEAD_DIM] = jnp.where(low_half, qp, 0.0).astype(BF16)
             qt[g, u * ROWS + HEAD_DIM : (u + 1) * ROWS] = jnp.where(
                 low_half, pltpu.roll(qp, HEAD_DIM, 1), 0.0
             ).astype(BF16)
-        mx_ref[g] = jnp.full((SPAN, ROWS), NEGATIVE, F32)
-        sum_ref[g] = jnp.zeros((SPAN, ROWS), F32)
-        pv_ref[g] = jnp.zeros((SPAN, ROWS), F32)
+        mx_ref[g] = jnp.full((2, 1, HALF), NEGATIVE, F32)
+        sum_ref[g] = jnp.zeros((2, 8, HALF), F32)
+        pv_ref[g] = jnp.zeros((2, HEAD_DIM, HALF), F32)
         forwarded(g).wait_recv()
+        for uh in range(2):
+            for par in range(2):
+                block = got[par, pl.ds(4 * g + 2 * uh, 2), 0:ROWS, :].reshape(HALF, ROWS)
+                turned = jnp.transpose(block.astype(F32))[HEAD_DIM:]
+                at = (2 * uh + par) * HALF
+                vt[g, :, at : at + HALF] = turned.astype(BF16)
 
         def visit(m, inner):
             other = lax.rem(start + m, 4)
@@ -380,6 +425,12 @@
             def _():
                 finish(gq)
 
+            @pl.when(jnp.logical_and(m == 0, p < 3))
+            def _():
+                ahead = lax.rem(start + p + 1, 4)
+                arrival(ahead)
+                forward(ahead).start()
+
             return inner
 
         lax.fori_loop(0, p + 1, visit, 0)
@@ -387,12 +438,9 @@
 
     @pl.when(is_head)
     def _():
+        arrival(start)
+        forward(start).start()
         lax.fori_loop(0, 4, phase, 0)
-
-    swap.wait_recv()
-    share = wide.at[half_rows, pl.ds(SHARE, SHARE)]
-    pass_on = rcopy(share, share, w_sem.at[2], w_sem.at[3], c=1 - c)
-    pass_on.start()
 
     @pl.when(is_head)
     def _():
@@ -405,18 +453,11 @@
 
     for fetch in fetches[5:]:
         fetch.wait()
-    for pair in range(HEADS // 2):
-        at = slice(pair * ROWS, (pair + 1) * ROWS)
-        even = att[2 * pair].astype(F32)
-        odd = att[2 * pair + 1].astype(F32)
-        attended[0:HEAD_DIM, at] = jnp.where(
-            low_half, even, pltpu.roll(odd, HEAD_DIM, 1)
-        ).astype(BF16)
-        attended[HEAD_DIM:ROWS, at] = jnp.where(
-            low_half, pltpu.roll(even, HEAD_DIM, 1), odd
-        ).astype(BF16)
-    residual = hid_ref[...].astype(F32) + jnp.dot(
-        attended[...], ow_ref[...], preferred_element_type=F32
+    residual = hid_ref[...].astype(F32) + lax.dot_general(
+        att[...].reshape(D, ROWS),
+        ow_ref[...],
+        (((0,), (0,)), ((), ())),
+        preferred_element_type=F32,
     )
     center = residual - jnp.sum(residual, axis=1, keepdims=True) * (1.0 / D)
     spread = jnp.sum(center * center, axis=1, keepdims=True) * (1.0 / D)
@@ -448,6 +489,10 @@
     row_copy(4).start()
     row_copy(5).start()
     row_copy(0).start()
+    swap.wait_recv()
+    share = wide.at[half_rows, pl.ds(SHARE, SHARE)]
+    pass_on = rcopy(share, share, w_sem.at[2], w_sem.at[3], c=1 - c)
+    pass_on.start()
     mine.wait()
     pass_on.wait_recv()
 
@@ -456,17 +501,7 @@
     diagonal = lane == rows_of((ROWS, ROWS))
     other = xl * 8 + z_pair
 
-    def stat_copy(slot):
-        side = lax.rem(slot, 2)
-        back = lax.rem(z - sig * (slot // 2) + 8, 8)
-        return rcopy(
-            stat_out.at[slot],
-            stats.at[xl * 4 + z // 2],
-            s_send.at[0],
-            s_recv.at[0],
-            xl=lax.rem(xl + side, 2),
-            z=back,
-        )
+    slot_j = (xl * 4 + z // 2) * 8
 
     def as_row(column):
         return jnp.sum(jnp.where(diagonal, column, 0.0), axis=0, keepdims=True)
@@ -525,58 +560,61 @@
         place = jnp.concatenate([placed(2 * n), placed(2 * n + 1)], axis=0)
         top = jnp.max(top, axis=1, keepdims=True)
         top2 = jnp.broadcast_to(top * LOG2E, (2 * ROWS, ROWS))
-        sum_ref[0, 0 : 2 * ROWS] = jnp.zeros((2 * ROWS, ROWS), F32)
-        pv_ref[0, 0 : 2 * ROWS] = jnp.zeros((2 * ROWS, ROWS), F32)
+        v_sum[...] = jnp.zeros((2 * ROWS, ROWS), F32)
+        v_pick[...] = jnp.zeros((2 * ROWS, ROWS), F32)
 
         def add_up(k, inner):
-            total = sum_ref[0, 0 : 2 * ROWS]
-            pick = pv_ref[0, 0 : 2 * ROWS]
+            total = v_sum[...]
+            pick = v_pick[...]
             for g in range(TILE // ROWS):
                 s = logit[k, :, g * ROWS : (g + 1) * ROWS]
                 total = total + jnp.exp2(s * LOG2E - top2)
                 pick = pick + jnp.where(place == k * TILE + g * ROWS, s, 0.0)
-            sum_ref[0, 0 : 2 * ROWS] = total
-            pv_ref[0, 0 : 2 * ROWS] = pick
+            v_sum[...] = total
+            v_pick[...] = pick
             return inner
 
         lax.fori_loop(0, TILES, add_up, 0)
-        lse = top + jnp.log(jnp.sum(sum_ref[0, 0 : 2 * ROWS], axis=1, keepdims=True))
-        pick = jnp.sum(pv_ref[0, 0 : 2 * ROWS], axis=1, keepdims=True)
-        row8 = rows_of((8, ROWS))
-        tiles = [
-            jnp.where(row8 == 0, as_row(lse[at : at + ROWS]), as_row(pick[at : at + ROWS]))
-            for at in (0, ROWS)
-        ]
-        stat_out[2 * n + 1] = tiles[1]
-        stat_copy(2 * n + 1).start()
-
-        @pl.when(n != 0)
-        def _():
-            stat_out[2 * n] = tiles[0]
-            stat_copy(2 * n).start()
-
-        @pl.when(n == 0)
-        def _():
-            stats[xl * 4 + z // 2] = tiles[0]
+        lse = top + jnp.log(jnp.sum(v_sum[...], axis=1, keepdims=True))
+        pick = jnp.sum(v_pick[...], axis=1, keepdims=True)
+        row2 = rows_of((2, ROWS))
+        for side in range(2):
+            at = slice(side * ROWS, (side + 1) * ROWS)
+            stat_out[n, lax.rem(xl + side, 2)] = jnp.where(
+                row2 == 0, as_row(lse[at]), as_row(pick[at])
+            )
+        spot = slot_j + lax.rem(z - sig * n + 8, 8)
+        stats[spot] = stat_out[n]
+        for k in range(1, DOCS):
+            rcopy(
+                stat_out.at[n], stats.at[spot], s_send.at[0], s_recv.at[0], **peer_doc(k)
+            ).start()
 
         return carry
 
     lax.fori_loop(0, 4, score_rows, 0)
 
-    part = stats.at[pl.ds(0, 7)]
-    rcopy(part, part, s_send.at[0], s_recv.at[0], z=z_dn).wait_recv()
-    parts = [stats[n] for n in range(8)]
-    top = parts[0][0:1]
-    for part in parts[1:]:
-        top = jnp.maximum(top, part[0:1])
-    total = jnp.zeros((1, ROWS), F32)
-    pick = jnp.zeros((1, ROWS), F32)
-    for part in parts:
-        total = total + jnp.exp(part[0:1] - top)
-        pick = pick + part[1:2]
-    place = seq * ROWS + lanes((1, ROWS))
-    nll = jnp.where(place < lengths_ref[doc], top + jnp.log(total) - pick, 0.0)
-    seqs[seq] = jnp.broadcast_to(jnp.sum(nll, axis=1, keepdims=True), (1, ROWS))
+    sent = stats.at[pl.ds(0, 60)]
+    rcopy(sent, sent, s_send.at[0], s_recv.at[0], z=z_dn).wait_recv()
+    entries = stats[...].reshape(8, DOCS, 2, ROWS)
+    top = jnp.max(entries, axis=0)
+    total = jnp.sum(jnp.exp(entries - top[None]), axis=0)
+    pick = jnp.sum(entries, axis=0)
+    shape = (DOCS, ROWS)
+    row = rows_of(shape)
+    col = lanes(shape)
+    scored = jnp.where(
+        rows_of((DOCS, 2, ROWS)) == 0, top + jnp.log(total), -pick
+    )
+    scored = jnp.sum(scored, axis=1)
+    limit = jnp.zeros(shape, jnp.int32)
+    for d in range(DOCS):
+        limit = jnp.where(row == d, lengths_ref[(d % 2) * 8 + d // 2], limit)
+    scored = jnp.where(seq * ROWS + col < limit, scored, 0.0)
+    nll = jnp.sum(jnp.where(row == 2 * z + xl, scored, 0.0), axis=0, keepdims=True)
+    doc_of = lax.rem(row, 2) * 8 + lax.div(row, 2)
+    sums = jnp.sum(scored, axis=1, keepdims=True)
+    seqs[seq] = jnp.sum(jnp.where(col == doc_of, sums, 0.0), axis=0, keepdims=True)
 
     for k in range(1, SEQ):
         rcopy(seqs.at[seq], seqs.at[seq], q_send.at[0], q_recv.at[0], **peer_seq(k)).start()
@@ -594,32 +632,26 @@
     def _():
         rcopy(packed, packed, a_send.at[0], a_recv.at[0], xh=xh, y=y).wait_send()
 
+    @pl.when(relays)
+    def _():
+        tie_pass.wait_send()
+
     swap.wait_send()
     pass_on.wait_send()
     for n in range(9):
         row_copy(n).wait_send()
     part = tgts.at[pl.ds(1, 7)]
     rcopy(part, part, t_send.at[0], t_recv.at[0], z=z_dn).wait_send()
-    part = stat_out.at[pl.ds(1, 7)]
-    rcopy(part, part, s_send.at[0], s_recv.at[0], z=z_dn).wait_send()
+    rcopy(sent, sent, s_send.at[0], s_recv.at[0], z=z_dn).wait_send()
     others = seqs.at[pl.ds(0, SEQ - 1)]
     rcopy(others, others, q_send.at[0], q_recv.at[0], z=z_dn).wait_recv()
-    docs[doc] = jnp.sum(seqs[...], axis=0)
-
-    for k in range(1, DOCS):
-        rcopy(docs.at[doc], docs.at[doc], d_send.at[0], d_recv.at[0], **peer_doc(k)).start()
-    rcopy(others, others, q_send.at[0], q_recv.at[0], z=z_dn).wait_send()
-    part = docs.at[pl.ds(0, DOCS - 1)]
-    rcopy(part, part, d_send.at[0], d_recv.at[0], z=z_dn).wait_recv()
-
-    shape = (DOCS, ROWS)
-    row = rows_of(shape)
-    col = lanes(shape)
-    column = docs[...].reshape(DOCS, ROWS)
+    line = jnp.sum(seqs[...], axis=0)
+    valid = lanes((1, ROWS)) < DOCS
+    count = jnp.ones((1, ROWS), F32)
     for d in range(DOCS):
-        column = jnp.where(row == d, column / lengths_ref[d].astype(F32), column)
-    valid = lanes((1, ROWS)) < DOCS
-    line = jnp.sum(jnp.where(row == col, column, 0.0), axis=0, keepdims=True)
+        count = jnp.where(lanes((1, ROWS)) == d, lengths_ref[d].astype(F32), count)
+    line = line / count
+    column = jnp.sum(jnp.where(row == col, line, 0.0), axis=1, keepdims=True)
     mean = jnp.sum(line, axis=1, keepdims=True) * (1.0 / DOCS)
     off = jnp.where(valid, line - mean, 0.0)
     spread = jnp.sqrt(jnp.sum(off * off, axis=1, keepdims=True) * (1.0 / DOCS) + SPREAD_EPSILON)
@@ -639,7 +671,7 @@
     accepted = jax.nn.sigmoid((level - line) / spread)
     row = rows_of((8, ROWS))
     final_ref[...] = jnp.where(row == 0, nll, jnp.where(row == 1, line, accepted))
-    rcopy(part, part, d_send.at[0], d_recv.at[0], z=z_dn).wait_send()
+    rcopy(others, others, q_send.at[0], q_recv.at[0], z=z_dn).wait_send()
 
 
 def split_kernel(final_ref, nll_ref, ppl_ref, acc_ref):
@@ -695,21 +727,22 @@
             pltpu.VMEM((2, 16, ROWS + HEAD_DIM, ROWS), BF16),
             pltpu.VMEM((16, HEAD_DIM, ROWS), BF16),
             pltpu.VMEM((HEADS, HEAD_DIM, ROWS), BF16),
-            pltpu.VMEM((ROWS, D), BF16),
             pltpu.VMEM((4, SPAN, ROWS), BF16),
-            pltpu.VMEM((SPAN, CHUNK), F32),
-            pltpu.VMEM((4, SPAN, ROWS), F32),
-            pltpu.VMEM((4, SPAN, ROWS), F32),
-            pltpu.VMEM((4, SPAN, ROWS), F32),
+            pltpu.VMEM((4, HEAD_DIM, 4 * HALF), BF16),
+            pltpu.VMEM((2, 4, HALF, HALF), F32),
+            pltpu.VMEM((4, 2, 1, HALF), F32),
+            pltpu.VMEM((4, 2, 8, HALF), F32),
+            pltpu.VMEM((4, 2, HEAD_DIM, HALF), F32),
+            pltpu.VMEM((2 * ROWS, ROWS), F32),
+            pltpu.VMEM((2 * ROWS, ROWS), F32),
             pltpu.VMEM((D, WIDE), BF16),
             pltpu.VMEM((8, ROWS, D), BF16),
             pltpu.VMEM((2, ROWS, D), BF16),
             pltpu.VMEM((TILES, 2 * ROWS, TILE), F32),
             pltpu.VMEM((8, 1, ROWS), jnp.int32),
-            pltpu.VMEM((8, 8, ROWS), F32),
-            pltpu.VMEM((8, 8, ROWS), F32),
+            pltpu.VMEM((4, 2, 2, ROWS), F32),
+            pltpu.VMEM((64, 2, 2, ROWS), F32),
             pltpu.VMEM((SEQ, 1, ROWS), F32),
-            pltpu.VMEM((DOCS, 1, ROWS), F32),
             dma((1,)),
             dma((4,)),
             dma((4,)),
@@ -725,9 +758,9 @@
             dma((1,)),
             dma((1,)),
             dma((1,)),
-            dma((1,)),
-            dma((1,)),
             dma((11,)),
+            pltpu.VMEM((ROWS + HEAD_DIM, ROWS), BF16),
+            dma((2,)),
         ],
         compiler_params=pltpu.CompilerParams(
             collective_id=0, has_side_effects=True, vmem_limit_bytes=67043328

time: 95.2 us -> 89.9 us (0.944)
  Pallas kernels: 93.8 us -> 88.5 us
    pallas_call x1, Pallas kernels: 92.6 us -> 87.3 us  [shards(): pl.pallas_call(kernel, name='scoring', out_shape=jax.ShapeDtypeStruct((8,...]
where the time goes in v3:
time: 89.9 us; the launch traced here: 89.8 us
  Pallas kernels  88.5 us (98%)
  between operations  1.29 us (1%)
    pallas_call x1, Pallas kernels, shards(): pl.pallas_call(kernel, name='scoring', out_shape=jax.ShapeDtypeStruct((8,...  87.3 us

profile of v3, /device:TPU:1, one launch (start us, length us, event | category | flops | bytes accessed | tf_op | source)
XLA Modules:
  0.0 89.8 jit_solution(6382116192428231093)
XLA Ops:
  1.3 87.3 %scoring.1.final_ref = f32[8,128]{1,0:T(8,128)} custom-call(f32[32,2,128]{2,1,0:T(2,128)} %constant.4.clone.base_in, f32[2,128,128]{2,1,0:T(8,128)} %constant.5.clone.step_in, s32[16]{0:T(128)} %lengths_in.1, s32[1]{0:T(128)S(6)} %copy.15.rank_in, bf16[128,768]{1,0:T(8,128)(2,1)} %bitcast.6, bf16[128,768]{1,0:T(8,128)(2,1)} %bitcast.7, ...), custom_call_target="tpu_custom_call" | custom-call | tf_op jit(solution)/shard_map/scoring/pallas_call | solution.py:709
  88.6 1.2 %split.1 = (f32[1,128]{1,0:T(1,128)}, f32[1,16]{1,0:T(1,128)}, f32[1,16]{1,0:T(1,128)}) custom-call(f32[8,128]{1,0:T(8,128)} %scoring.1.final_ref), custom_call_target="tpu_custom_call" | custom-call | tf_op jit(solution)/shard_map/split/pallas_call | solution.py:782

commit v4 on v3

--- a/solution.py
+++ b/solution.py
@@ -202,15 +202,17 @@
 
     pl.semaphore_wait(barrier, SEQ - 1 + DOCS - 1)
 
-    half_rows = pl.ds(pl.multiple_of(c * (D // 2), D // 2), D // 2)
-    swap = rcopy(
-        un_ref.at[half_rows],
-        wide.at[half_rows, pl.ds(SHARE, SHARE)],
-        w_sem.at[0],
-        w_sem.at[1],
-        z=z_pair,
-    )
-    swap.start()
+    swaps = []
+    passes = []
+    for n, (start_row, count) in enumerate(((0, 288), (288, 96))):
+        some = pl.ds(pl.multiple_of(c * (D // 2) + start_row, 32), count)
+        landing = wide.at[some, pl.ds(SHARE, SHARE)]
+        swaps.append(
+            rcopy(un_ref.at[some], landing, w_sem.at[n], w_sem.at[2 + n], z=z_pair)
+        )
+        passes.append(rcopy(landing, landing, w_sem.at[5 + n], w_sem.at[7 + n], c=1 - c))
+    for swap in swaps:
+        swap.start()
 
     is_head = jnp.logical_and(y != 3, y != 7)
     my_slot = y - jnp.where(y > 3, 1, 0)
@@ -442,6 +444,10 @@
         forward(start).start()
         lax.fori_loop(0, 4, phase, 0)
 
+    for swap, pass_on in zip(swaps, passes):
+        swap.wait_recv()
+        pass_on.start()
+
     @pl.when(is_head)
     def _():
         part = att.at[pl.ds(0, HEADS - 1)]
@@ -463,38 +469,47 @@
     spread = jnp.sum(center * center, axis=1, keepdims=True) * (1.0 / D)
     rows_buf[0] = (center * lax.rsqrt(spread + NORM_EPSILON) * gain_ref[...].reshape(1, D)).astype(BF16)
 
-    def row_copy(n):
+    def part_of(slot, h):
+        if slot >= 8:
+            return relay.at[slot - 8, pl.ds(h * HEAD_DIM, HEAD_DIM)]
+        return rows_buf.at[slot, pl.ds(h * HEAD_DIM, HEAD_DIM)]
+
+    def row_copy(n, h):
+        where = {"z": z_dn}
         if n < 4:
-            return rcopy(
-                rows_buf.at[2 * n],
-                rows_buf.at[2 * n + 1],
-                c_send.at[n],
-                c_recv.at[2 * n + 1],
-                xl=1 - xl,
-            )
-        if n == 4:
-            return rcopy(rows_buf.at[0], rows_buf.at[2], c_send.at[4], c_recv.at[2], z=z_dn)
-        if n == 5:
-            return rcopy(rows_buf.at[0], relay.at[0], c_send.at[5], c_recv.at[8], z=z_up)
-        if n == 6:
-            return rcopy(rows_buf.at[2], relay.at[1], c_send.at[6], c_recv.at[9], z=z_up)
-        if n == 7:
-            return rcopy(relay.at[0], rows_buf.at[4], c_send.at[7], c_recv.at[4], z=z_dn)
-        return rcopy(relay.at[1], rows_buf.at[6], c_send.at[8], c_recv.at[6], z=z_dn)
-
-    def row_wait(slot):
-        ref = relay.at[slot - 8] if slot >= 8 else rows_buf.at[slot]
-        rcopy(rows_buf.at[0], ref, c_send.at[0], c_recv.at[slot], z=z_dn).wait_recv()
-
-    row_copy(4).start()
-    row_copy(5).start()
-    row_copy(0).start()
-    swap.wait_recv()
-    share = wide.at[half_rows, pl.ds(SHARE, SHARE)]
-    pass_on = rcopy(share, share, w_sem.at[2], w_sem.at[3], c=1 - c)
-    pass_on.start()
+            source, target = 2 * n, 2 * n + 1
+            where = {"xl": 1 - xl}
+        elif n == 4:
+            source, target = 0, 2
+        elif n == 5:
+            source, target = 0, 8
+            where = {"z": z_up}
+        elif n == 6:
+            source, target = 2, 9
+            where = {"z": z_up}
+        elif n == 7:
+            source, target = 8, 4
+        else:
+            source, target = 9, 6
+        return rcopy(
+            part_of(source, h),
+            part_of(target, h),
+            c_send.at[2 * n + h],
+            c_recv.at[2 * target + h],
+            **where,
+        )
+
+    def row_wait(slot, h):
+        part = part_of(slot, h)
+        rcopy(part, part, c_send.at[0], c_recv.at[2 * slot + h], z=z_dn).wait_recv()
+
+    for h in range(2):
+        row_copy(4, h).start()
+        row_copy(5, h).start()
+        row_copy(0, h).start()
     mine.wait()
-    pass_on.wait_recv()
+    for pass_on in passes:
+        pass_on.wait_recv()
 
     part = tgts.at[pl.ds(1, 7)]
     rcopy(part, part, t_send.at[0], t_recv.at[0], z=z_dn).wait_recv()
@@ -507,35 +522,52 @@
         return jnp.sum(jnp.where(diagonal, column, 0.0), axis=0, keepdims=True)
 
     def score_rows(n, carry):
-        @pl.when(n == 0)
-        def _():
-            row_wait(1)
-            row_wait(2)
-            row_copy(6).start()
-            row_copy(1).start()
-            row_wait(8)
-            row_copy(7).start()
-
         @pl.when(n == 1)
         def _():
-            row_wait(9)
-            row_copy(8).start()
-            row_wait(4)
-            row_copy(2).start()
-            row_wait(3)
+            for h in range(2):
+                row_wait(8, h)
+                row_copy(7, h).start()
+                row_wait(2, h)
+                row_copy(6, h).start()
+                row_copy(1, h).start()
+            for h in range(2):
+                row_wait(1, h)
 
         @pl.when(n == 2)
         def _():
-            row_wait(6)
-            row_copy(3).start()
-            row_wait(5)
+            row_wait(9, 0)
+            row_copy(8, 0).start()
+            row_wait(4, 0)
+            row_copy(2, 0).start()
 
         @pl.when(n == 3)
         def _():
-            row_wait(7)
-
-        block = rows_buf[pl.ds(2 * n, 2)].reshape(2 * ROWS, D)
-        top = jnp.full((2 * ROWS, ROWS), NEGATIVE, F32)
+            row_wait(9, 1)
+            row_copy(8, 1).start()
+            row_wait(4, 1)
+            row_copy(2, 1).start()
+            for h in range(2):
+                row_wait(3, h)
+
+        @pl.when(n == 4)
+        def _():
+            row_wait(6, 0)
+            row_copy(3, 0).start()
+
+        @pl.when(n == 5)
+        def _():
+            row_wait(6, 1)
+            row_copy(3, 1).start()
+            for h in range(2):
+                row_wait(5, h)
+
+        @pl.when(n == 7)
+        def _():
+            for h in range(2):
+                row_wait(7, h)
+
+        block = rows_buf[n]
+        top = jnp.full((ROWS, ROWS), NEGATIVE, F32)
         for k in range(TILES):
             s = jnp.dot(
                 block, wide[:, k * TILE : (k + 1) * TILE], preferred_element_type=F32
@@ -543,25 +575,22 @@
             logit[k] = s
             top = jnp.maximum(top, jnp.maximum(s[:, :ROWS], s[:, ROWS:]))
 
-        def placed(slot):
-            wanted = jnp.broadcast_to(tgts[slot], (ROWS, ROWS))
-            wanted = jnp.sum(
-                jnp.where(diagonal, wanted.astype(F32), 0.0), axis=1, keepdims=True
-            ).astype(jnp.int32)
-            here = wanted - doc * SHARE
-            there = wanted - other * SHARE
-            spot = jnp.where(
-                jnp.logical_and(here >= 0, here < SHARE),
-                here,
-                jnp.where(jnp.logical_and(there >= 0, there < SHARE), there + SHARE, -1),
-            )
-            return jnp.broadcast_to(spot, (ROWS, ROWS)) - lane
-
-        place = jnp.concatenate([placed(2 * n), placed(2 * n + 1)], axis=0)
+        wanted = jnp.broadcast_to(tgts[n], (ROWS, ROWS))
+        wanted = jnp.sum(
+            jnp.where(diagonal, wanted.astype(F32), 0.0), axis=1, keepdims=True
+        ).astype(jnp.int32)
+        here = wanted - doc * SHARE
+        there = wanted - other * SHARE
+        place = jnp.where(
+            jnp.logical_and(here >= 0, here < SHARE),
+            here,
+            jnp.where(jnp.logical_and(there >= 0, there < SHARE), there + SHARE, -1),
+        )
+        place = jnp.broadcast_to(place, (ROWS, ROWS)) - lane
         top = jnp.max(top, axis=1, keepdims=True)
-        top2 = jnp.broadcast_to(top * LOG2E, (2 * ROWS, ROWS))
-        v_sum[...] = jnp.zeros((2 * ROWS, ROWS), F32)
-        v_pick[...] = jnp.zeros((2 * ROWS, ROWS), F32)
+        top2 = jnp.broadcast_to(top * LOG2E, (ROWS, ROWS))
+        v_sum[...] = jnp.zeros((ROWS, ROWS), F32)
+        v_pick[...] = jnp.zeros((ROWS, ROWS), F32)
 
         def add_up(k, inner):
             total = v_sum[...]
@@ -577,22 +606,18 @@
         lax.fori_loop(0, TILES, add_up, 0)
         lse = top + jnp.log(jnp.sum(v_sum[...], axis=1, keepdims=True))
         pick = jnp.sum(v_pick[...], axis=1, keepdims=True)
-        row2 = rows_of((2, ROWS))
-        for side in range(2):
-            at = slice(side * ROWS, (side + 1) * ROWS)
-            stat_out[n, lax.rem(xl + side, 2)] = jnp.where(
-                row2 == 0, as_row(lse[at]), as_row(pick[at])
-            )
-        spot = slot_j + lax.rem(z - sig * n + 8, 8)
-        stats[spot] = stat_out[n]
+        stat_out[n] = jnp.where(rows_of((2, ROWS)) == 0, as_row(lse), as_row(pick))
+        spot = slot_j + lax.rem(z - sig * lax.div(n, 2) + 8, 8)
+        plane = lax.rem(xl + n, 2)
+        stats[spot, plane] = stat_out[n]
         for k in range(1, DOCS):
             rcopy(
-                stat_out.at[n], stats.at[spot], s_send.at[0], s_recv.at[0], **peer_doc(k)
+                stat_out.at[n], stats.at[spot, plane], s_send.at[0], s_recv.at[0], **peer_doc(k)
             ).start()
 
         return carry
 
-    lax.fori_loop(0, 4, score_rows, 0)
+    lax.fori_loop(0, 8, score_rows, 0)
 
     sent = stats.at[pl.ds(0, 60)]
     rcopy(sent, sent, s_send.at[0], s_recv.at[0], z=z_dn).wait_recv()
@@ -636,10 +661,11 @@
     def _():
         tie_pass.wait_send()
 
-    swap.wait_send()
-    pass_on.wait_send()
+    for copy in swaps + passes:
+        copy.wait_send()
     for n in range(9):
-        row_copy(n).wait_send()
+        for h in range(2):
+            row_copy(n, h).wait_send()
     part = tgts.at[pl.ds(1, 7)]
     rcopy(part, part, t_send.at[0], t_recv.at[0], z=z_dn).wait_send()
     rcopy(sent, sent, s_send.at[0], s_recv.at[0], z=z_dn).wait_send()
@@ -733,14 +759,14 @@
             pltpu.VMEM((4, 2, 1, HALF), F32),
             pltpu.VMEM((4, 2, 8, HALF), F32),
             pltpu.VMEM((4, 2, HEAD_DIM, HALF), F32),
-            pltpu.VMEM((2 * ROWS, ROWS), F32),
-            pltpu.VMEM((2 * ROWS, ROWS), F32),
+            pltpu.VMEM((ROWS, ROWS), F32),
+            pltpu.VMEM((ROWS, ROWS), F32),
             pltpu.VMEM((D, WIDE), BF16),
             pltpu.VMEM((8, ROWS, D), BF16),
             pltpu.VMEM((2, ROWS, D), BF16),
-            pltpu.VMEM((TILES, 2 * ROWS, TILE), F32),
+            pltpu.VMEM((TILES, ROWS, TILE), F32),
             pltpu.VMEM((8, 1, ROWS), jnp.int32),
-            pltpu.VMEM((4, 2, 2, ROWS), F32),
+            pltpu.VMEM((8, 2, ROWS), F32),
             pltpu.VMEM((64, 2, 2, ROWS), F32),
             pltpu.VMEM((SEQ, 1, ROWS), F32),
             dma((1,)),
@@ -749,9 +775,9 @@
             dma((4,)),
             dma((1,)),
             dma((1,)),
-            dma((5,)),
             dma((9,)),
-            dma((10,)),
+            dma((18,)),
+            dma((20,)),
             dma((1,)),
             dma((1,)),
             dma((1,)),

time: 89.9 us -> 86.2 us (0.959)
  Pallas kernels: 88.5 us -> 84.8 us
    pallas_call x1, Pallas kernels: 87.3 us -> 83.6 us  [shards(): pl.pallas_call(kernel, name='scoring', out_shape=jax.ShapeDtypeStruct((8,...]
where the time goes in v4:
time: 86.2 us; the launch traced here: 86.1 us
  Pallas kernels  84.8 us (98%)
  between operations  1.29 us (1%)
    pallas_call x1, Pallas kernels, shards(): pl.pallas_call(kernel, name='scoring', out_shape=jax.ShapeDtypeStruct((8,...  83.6 us

profile of v4, /device:TPU:1, one launch (start us, length us, event | category | flops | bytes accessed | tf_op | source)
XLA Modules:
  0.0 86.1 jit_solution(11652153028727232343)
XLA Ops:
  1.3 83.6 %scoring.1.final_ref = f32[8,128]{1,0:T(8,128)} custom-call(f32[32,2,128]{2,1,0:T(2,128)} %constant.4.clone.base_in, f32[2,128,128]{2,1,0:T(8,128)} %constant.5.clone.step_in, s32[16]{0:T(128)} %lengths_in.1, s32[1]{0:T(128)S(6)} %copy.15.rank_in, bf16[128,768]{1,0:T(8,128)(2,1)} %bitcast.6, bf16[128,768]{1,0:T(8,128)(2,1)} %bitcast.7, ...), custom_call_target="tpu_custom_call" | custom-call | tf_op jit(solution)/shard_map/scoring/pallas_call | solution.py:735
  84.9 1.2 %split.1 = (f32[1,128]{1,0:T(1,128)}, f32[1,16]{1,0:T(1,128)}, f32[1,16]{1,0:T(1,128)}) custom-call(f32[8,128]{1,0:T(8,128)} %scoring.1.final_ref), custom_call_target="tpu_custom_call" | custom-call | tf_op jit(solution)/shard_map/split/pallas_call | solution.py:808

commit v5 on v4

--- a/solution.py
+++ b/solution.py
@@ -129,18 +129,22 @@
 
     barrier = pltpu.get_barrier_semaphore()
 
-    def peer_seq(k):
-        n = lax.rem(seq + k, SEQ)
-        return {"xh": lax.div(n, 16), "y": lax.rem(lax.div(n, 2), 8), "c": lax.rem(n, 2)}
-
-    def peer_doc(k):
-        n = lax.rem(doc + k, DOCS)
-        return {"xl": lax.div(n, 8), "z": lax.rem(n, 8)}
-
-    for k in range(1, SEQ):
-        pl.semaphore_signal(barrier, inc=1, device_id=peer_seq(k), device_id_type=MESH)
-    for k in range(1, DOCS):
-        pl.semaphore_signal(barrier, inc=1, device_id=peer_doc(k), device_id_type=MESH)
+    xh_at, c_at, xl_at = [xh, 1 - xh], [c, 1 - c], [xl, 1 - xl]
+    y_at = [y] + [lax.rem(y + k, 8) for k in range(1, 8)]
+    z_at = [z] + [lax.rem(z + k, 8) for k in range(1, 8)]
+    far_first = (4, 3, 5, 2, 6, 1, 7, 0)
+    seq_peers = [
+        {"xh": xh_at[i], "y": y_at[j], "c": c_at[k]}
+        for i in (1, 0)
+        for j in far_first
+        for k in (0, 1)
+        if i or j or k
+    ]
+    doc_peers = [
+        {"xl": xl_at[i], "z": z_at[j]} for j in far_first for i in (1, 0) if i or j
+    ]
+    for where in seq_peers + doc_peers:
+        pl.semaphore_signal(barrier, inc=1, device_id=where, device_id_type=MESH)
 
     fetches = [
         pltpu.make_async_copy(src, dst, i_sem.at[n])
@@ -211,22 +215,22 @@
             rcopy(un_ref.at[some], landing, w_sem.at[n], w_sem.at[2 + n], z=z_pair)
         )
         passes.append(rcopy(landing, landing, w_sem.at[5 + n], w_sem.at[7 + n], c=1 - c))
-    for swap in swaps:
-        swap.start()
-
     is_head = jnp.logical_and(y != 3, y != 7)
     my_slot = y - jnp.where(y > 3, 1, 0)
     my_head = jnp.where(is_head, xh * 6 + my_slot, -1)
 
     start = lax.rem(my_head, 4)
     my_group = lax.div(me, 4)
+
+    def turn_of(h):
+        return lax.rem(my_group + 4 - lax.rem(h, 4), 4)
 
     def head_copy(h):
         yi = lax.rem(h, 6)
         return rcopy(
             packed.at[h],
             got.at[c, me],
-            a_send.at[0],
+            a_send.at[turn_of(h)],
             a_recv.at[my_group],
             xh=h // 6,
             y=yi + jnp.where(yi > 2, 1, 0),
@@ -240,7 +244,7 @@
     tie_send = rcopy(
         packed.at[jnp.maximum(tie_head, 0)],
         tie_buf,
-        a_send.at[0],
+        a_send.at[turn_of(jnp.maximum(tie_head, 0))],
         tie_sem.at[0],
         xh=xh,
         y=lax.rem(y + 5, 8),
@@ -254,6 +258,9 @@
         y=lax.rem(y + 7, 8),
     )
 
+    for swap in swaps:
+        swap.start()
+
     @pl.when(has_tie)
     def _():
         tie_send.start()
@@ -271,7 +278,24 @@
 
         return carry
 
-    lax.fori_loop(0, HEADS, send_head, 0)
+    lax.fori_loop(0, HEADS // 2, send_head, 0)
+
+    @pl.when(relays)
+    def _():
+        tie_send.wait_recv()
+        tie_pass.start()
+
+    own_turn = jnp.where(is_head, turn_of(jnp.maximum(my_head, 0)), -1)
+
+    def sent_turn(p):
+        for count in (2, 3):
+            @pl.when((own_turn == p) if count == 2 else (own_turn != p))
+            def _():
+                part = packed.at[pl.ds(0, count)]
+                rcopy(part, part, a_send.at[p], a_recv.at[0], xh=xh, y=y).wait_send()
+
+    sent_turn(0)
+    lax.fori_loop(HEADS // 2, HEADS, send_head, 0)
 
     def target_copy(n):
         side = lax.rem(n, 2)
@@ -294,11 +318,6 @@
 
     lax.fori_loop(1, 8, send_target, 0)
 
-    @pl.when(relays)
-    def _():
-        tie_send.wait_recv()
-        tie_pass.start()
-
     def arrival(g):
         def wait(count):
             part = got.at[c, pl.ds(4 * g, count)]
@@ -333,45 +352,64 @@
         )
 
     def pair_of(gq, gk, diagonal):
-        blocks = [(uh, par) for uh in range(2) for par in range(2)]
-        tops = []
-        for hq in range(2):
-            queries = qt[gq, hq * HALF : (hq + 1) * HALF]
-            top = jnp.full((8, HALF), NEGATIVE, F32)
-            for b, (uh, par) in enumerate(blocks):
-                if diagonal and uh > hq:
-                    continue
-                keys = got[par, pl.ds(4 * gk + 2 * uh, 2), 0:ROWS, :].reshape(HALF, ROWS)
-                s = lax.dot_general(
-                    keys, queries, (((1,), (1,)), ((), ())), preferred_element_type=F32
-                )
-                if diagonal and uh == hq:
-                    row = rows_of((HALF, HALF))
-                    col = lanes((HALF, HALF))
-                    key = row + jnp.where(row >= ROWS, ROWS, 0) + par * ROWS
-                    query = col + jnp.where(col >= ROWS, ROWS, 0) + c * ROWS
-                    s = jnp.where(key <= query, s, NEGATIVE)
-                s_scr[hq, b] = s
-                top = jnp.maximum(top, jnp.max(s.reshape(HALF // 8, 8, HALF), axis=0))
-            tops.append(top)
-        for hq in range(2):
+        counts = [2, 4] if diagonal else [4, 4]
+
+        def score(hq, b):
+            uh, par = b // 2, b % 2
+            keys = got[par, pl.ds(4 * gk + 2 * uh, 2), 0:ROWS, :].reshape(HALF, ROWS)
+            s = lax.dot_general(
+                keys,
+                qt[gq, hq * HALF : (hq + 1) * HALF],
+                (((1,), (1,)), ((), ())),
+                preferred_element_type=F32,
+            )
+            if diagonal and uh == hq:
+                row = rows_of((HALF, HALF))
+                col = lanes((HALF, HALF))
+                key = row + jnp.where(row >= ROWS, ROWS, 0) + par * ROWS
+                query = col + jnp.where(col >= ROWS, ROWS, 0) + c * ROWS
+                s = jnp.where(key <= query, s, NEGATIVE)
+            s_scr[hq, b] = s
+            return jnp.max(s.reshape(HALF // 8, 8, HALF), axis=0)
+
+        def raise_top(hq, top):
             old = mx_ref[gq, hq]
-            new = jnp.maximum(old, jnp.max(tops[hq], axis=0, keepdims=True) * scale)
+            new = jnp.maximum(old, jnp.max(top, axis=0, keepdims=True) * scale)
             mx_ref[gq, hq] = new
-            factor = jnp.exp2(old - new)
-            total = sum_ref[gq, hq] * factor
-            parts = []
-            count = 2 if diagonal and hq == 0 else 4
-            for b in range(count):
-                p = jnp.exp2(s_scr[hq, b] * scale - new)
-                total = total + jnp.sum(p.reshape(HALF // 8, 8, HALF), axis=0)
-                parts.append(p.astype(BF16))
-            sum_ref[gq, hq] = total
+            return new, jnp.exp2(old - new)
+
+        def weigh(hq, b, new):
+            p = jnp.exp2(s_scr[hq, b] * scale - new)
+            return p.astype(BF16), jnp.sum(p.reshape(HALF // 8, 8, HALF), axis=0)
+
+        def close(hq, parts, total, factor):
+            sum_ref[gq, hq] = sum_ref[gq, hq] * factor + total
             pv_ref[gq, hq] = pv_ref[gq, hq] * factor + jnp.dot(
-                vt[gk, :, 0 : count * HALF],
+                vt[gk, :, 0 : len(parts) * HALF],
                 jnp.concatenate(parts, axis=0),
                 preferred_element_type=F32,
             )
+
+        top = score(0, 0)
+        for b in range(1, counts[0]):
+            top = jnp.maximum(top, score(0, b))
+        new, factor = raise_top(0, top)
+        parts, total, top = [], 0.0, None
+        for b in range(4):
+            part = score(1, b)
+            top = part if top is None else jnp.maximum(top, part)
+            if b < counts[0]:
+                p, add = weigh(0, b, new)
+                parts.append(p)
+                total = total + add
+        close(0, parts, total, factor)
+        new, factor = raise_top(1, top)
+        parts, total = [], 0.0
+        for b in range(counts[1]):
+            p, add = weigh(1, b, new)
+            parts.append(p)
+            total = total + add
+        close(1, parts, total, factor)
 
     def finish(gq):
         for hq in range(2):
@@ -610,9 +648,9 @@
         spot = slot_j + lax.rem(z - sig * lax.div(n, 2) + 8, 8)
         plane = lax.rem(xl + n, 2)
         stats[spot, plane] = stat_out[n]
-        for k in range(1, DOCS):
+        for where in doc_peers:
             rcopy(
-                stat_out.at[n], stats.at[spot, plane], s_send.at[0], s_recv.at[0], **peer_doc(k)
+                stat_out.at[n], stats.at[spot, plane], s_send.at[0], s_recv.at[0], **where
             ).start()
 
         return carry
@@ -641,21 +679,18 @@
     sums = jnp.sum(scored, axis=1, keepdims=True)
     seqs[seq] = jnp.sum(jnp.where(col == doc_of, sums, 0.0), axis=0, keepdims=True)
 
-    for k in range(1, SEQ):
-        rcopy(seqs.at[seq], seqs.at[seq], q_send.at[0], q_recv.at[0], **peer_seq(k)).start()
+    for where in seq_peers:
+        rcopy(seqs.at[seq], seqs.at[seq], q_send.at[0], q_recv.at[0], **where).start()
 
     @pl.when(is_head)
     def _():
-        part = packed.at[pl.ds(0, HEADS - 1)]
-        rcopy(part, part, a_send.at[0], a_recv.at[0], xh=xh, y=y).wait_send()
         part = outs.at[pl.ds(0, 15)]
         rcopy(part, part, r_send.at[0], r_recv.at[0], xh=xh, y=y).wait_send()
         for g in range(4):
             forward(g).wait_send()
 
-    @pl.when(jnp.logical_not(is_head))
-    def _():
-        rcopy(packed, packed, a_send.at[0], a_recv.at[0], xh=xh, y=y).wait_send()
+    for p in range(1, 4):
+        sent_turn(p)
 
     @pl.when(relays)
     def _():
@@ -685,7 +720,7 @@
         column < line, jnp.logical_and(column == line, row < col)
     )
     rank = jnp.sum(jnp.where(ahead, 1.0, 0.0), axis=0, keepdims=True)
-    scaled = rank_ref[0] * (DOCS - 1)
+    scaled = rank_ref[0, 0] * (DOCS - 1)
     low_index = lax.div(scaled, 99)
     high_index = jnp.minimum(low_index + 1, DOCS - 1)
     fraction = (scaled - 99 * low_index).astype(F32) / 99.0
@@ -742,7 +777,7 @@
             pltpu.VMEM((2, ROWS), F32),
             pltpu.VMEM((2, ROWS, ROWS), F32),
             pltpu.SMEM((DOCS,), jnp.int32),
-            pltpu.SMEM((1,), jnp.int32),
+            pltpu.SMEM((1, 1), jnp.int32),
             pltpu.VMEM((ROWS, D), BF16),
             pltpu.VMEM((ROWS, D), BF16),
             pltpu.VMEM((ROWS, D), BF16),
@@ -769,7 +804,7 @@
             pltpu.VMEM((8, 2, ROWS), F32),
             pltpu.VMEM((64, 2, 2, ROWS), F32),
             pltpu.VMEM((SEQ, 1, ROWS), F32),
-            dma((1,)),
+            dma((4,)),
             dma((4,)),
             dma((4,)),
             dma((4,)),
@@ -795,7 +830,7 @@
         jnp.asarray(base),
         jnp.asarray(step),
         lengths,
-        keep_rank,
+        keep_rank.reshape(1, 1),
         queries[0],
         key_states[0],
         values[0],

time: 86.2 us -> 86.7 us (level)
  no operation moved by 1% of the time
where the time goes in v5:
time: 86.7 us; the launch traced here: 86.5 us
  Pallas kernels  85.2 us (98%)
  between operations  1.29 us (1%)
    pallas_call x1, Pallas kernels, shards(): pl.pallas_call(kernel, name='scoring', out_shape=jax.ShapeDtypeStruct((8,...  84 us

profile of v5, /device:TPU:1, one launch (start us, length us, event | category | flops | bytes accessed | tf_op | source)
XLA Modules:
  0.0 86.5 jit_solution(17004590396955427034)
XLA Ops:
  1.3 84.0 %scoring.1.final_ref = f32[8,128]{1,0:T(8,128)} custom-call(f32[32,2,128]{2,1,0:T(2,128)} %constant.4.clone.base_in, f32[2,128,128]{2,1,0:T(8,128)} %constant.5.clone.step_in, s32[16]{0:T(128)} %lengths_in.1, s32[1,1]{1,0:T(1,128)} %bitcast.7.rank_in, bf16[128,768]{1,0:T(8,128)(2,1)} %bitcast.8, bf16[128,768]{1,0:T(8,128)(2,1)} %bitcast.9, ...), custom_call_target="tpu_custom_call" | custom-call | tf_op jit(solution)/shard_map/scoring/pallas_call | solution.py:770
  85.3 1.2 %split.1 = (f32[1,128]{1,0:T(1,128)}, f32[1,16]{1,0:T(1,128)}, f32[1,16]{1,0:T(1,128)}) custom-call(f32[8,128]{1,0:T(8,128)} %scoring.1.final_ref), custom_call_target="tpu_custom_call" | custom-call | tf_op jit(solution)/shard_map/split/pallas_call | solution.py:843

commit v6 on v5

--- a/solution.py
+++ b/solution.py
@@ -215,22 +215,22 @@
             rcopy(un_ref.at[some], landing, w_sem.at[n], w_sem.at[2 + n], z=z_pair)
         )
         passes.append(rcopy(landing, landing, w_sem.at[5 + n], w_sem.at[7 + n], c=1 - c))
+    for swap in swaps:
+        swap.start()
+
     is_head = jnp.logical_and(y != 3, y != 7)
     my_slot = y - jnp.where(y > 3, 1, 0)
     my_head = jnp.where(is_head, xh * 6 + my_slot, -1)
 
     start = lax.rem(my_head, 4)
     my_group = lax.div(me, 4)
-
-    def turn_of(h):
-        return lax.rem(my_group + 4 - lax.rem(h, 4), 4)
 
     def head_copy(h):
         yi = lax.rem(h, 6)
         return rcopy(
             packed.at[h],
             got.at[c, me],
-            a_send.at[turn_of(h)],
+            a_send.at[0],
             a_recv.at[my_group],
             xh=h // 6,
             y=yi + jnp.where(yi > 2, 1, 0),
@@ -244,7 +244,7 @@
     tie_send = rcopy(
         packed.at[jnp.maximum(tie_head, 0)],
         tie_buf,
-        a_send.at[turn_of(jnp.maximum(tie_head, 0))],
+        a_send.at[0],
         tie_sem.at[0],
         xh=xh,
         y=lax.rem(y + 5, 8),
@@ -258,9 +258,6 @@
         y=lax.rem(y + 7, 8),
     )
 
-    for swap in swaps:
-        swap.start()
-
     @pl.when(has_tie)
     def _():
         tie_send.start()
@@ -278,24 +275,7 @@
 
         return carry
 
-    lax.fori_loop(0, HEADS // 2, send_head, 0)
-
-    @pl.when(relays)
-    def _():
-        tie_send.wait_recv()
-        tie_pass.start()
-
-    own_turn = jnp.where(is_head, turn_of(jnp.maximum(my_head, 0)), -1)
-
-    def sent_turn(p):
-        for count in (2, 3):
-            @pl.when((own_turn == p) if count == 2 else (own_turn != p))
-            def _():
-                part = packed.at[pl.ds(0, count)]
-                rcopy(part, part, a_send.at[p], a_recv.at[0], xh=xh, y=y).wait_send()
-
-    sent_turn(0)
-    lax.fori_loop(HEADS // 2, HEADS, send_head, 0)
+    lax.fori_loop(0, HEADS, send_head, 0)
 
     def target_copy(n):
         side = lax.rem(n, 2)
@@ -317,6 +297,11 @@
         return carry
 
     lax.fori_loop(1, 8, send_target, 0)
+
+    @pl.when(relays)
+    def _():
+        tie_send.wait_recv()
+        tie_pass.start()
 
     def arrival(g):
         def wait(count):
@@ -684,13 +669,16 @@
 
     @pl.when(is_head)
     def _():
+        part = packed.at[pl.ds(0, HEADS - 1)]
+        rcopy(part, part, a_send.at[0], a_recv.at[0], xh=xh, y=y).wait_send()
         part = outs.at[pl.ds(0, 15)]
         rcopy(part, part, r_send.at[0], r_recv.at[0], xh=xh, y=y).wait_send()
         for g in range(4):
             forward(g).wait_send()
 
-    for p in range(1, 4):
-        sent_turn(p)
+    @pl.when(jnp.logical_not(is_head))
+    def _():
+        rcopy(packed, packed, a_send.at[0], a_recv.at[0], xh=xh, y=y).wait_send()
 
     @pl.when(relays)
     def _():
@@ -804,7 +792,7 @@
             pltpu.VMEM((8, 2, ROWS), F32),
             pltpu.VMEM((64, 2, 2, ROWS), F32),
             pltpu.VMEM((SEQ, 1, ROWS), F32),
-            dma((4,)),
+            dma((1,)),
             dma((4,)),
             dma((4,)),
             dma((4,)),

time: 86.7 us -> 86 us (level)
  no operation moved by 1% of the time
where the time goes in v6:
time: 86 us; the launch traced here: 85.8 us
  Pallas kernels  84.6 us (98%)
  between operations  1.29 us (2%)
    pallas_call x1, Pallas kernels, shards(): pl.pallas_call(kernel, name='scoring', out_shape=jax.ShapeDtypeStruct((8,...  83.4 us

profile of v6, /device:TPU:1, one launch (start us, length us, event | category | flops | bytes accessed | tf_op | source)
XLA Modules:
  0.0 85.8 jit_solution(12584728158919338106)
XLA Ops:
  1.3 83.4 %scoring.1.final_ref = f32[8,128]{1,0:T(8,128)} custom-call(f32[32,2,128]{2,1,0:T(2,128)} %constant.4.clone.base_in, f32[2,128,128]{2,1,0:T(8,128)} %constant.5.clone.step_in, s32[16]{0:T(128)} %lengths_in.1, s32[1,1]{1,0:T(1,128)} %bitcast.7.rank_in, bf16[128,768]{1,0:T(8,128)(2,1)} %bitcast.8, bf16[128,768]{1,0:T(8,128)(2,1)} %bitcast.9, ...), custom_call_target="tpu_custom_call" | custom-call | tf_op jit(solution)/shard_map/scoring/pallas_call | solution.py:758
  84.7 1.2 %split.1 = (f32[1,128]{1,0:T(1,128)}, f32[1,16]{1,0:T(1,128)}, f32[1,16]{1,0:T(1,128)}) custom-call(f32[8,128]{1,0:T(8,128)} %scoring.1.final_ref), custom_call_target="tpu_custom_call" | custom-call | tf_op jit(solution)/shard_map/split/pallas_call | solution.py:831
